TPU v7x, 32 devices: a whole 2x2x4 slice. The times are simulated.
32 devices in a mesh: stream: 4 (over y, x), span: 8 (over z, core).
Axes of the slice: x: 2, y: 2, z: 4, core: 2. Of those that a mesh axis runs over, the one named last changes fastest.
Arguments:
- fine_pops: float32 [27, 24, 48, 128], P(None, 'stream', 'span'), may hold values from 0.5 to 2
- coarse_pops: float32 [27, 12, 24, 64], P(None, 'stream', 'span'), may hold values from 0.5 to 2
- obstacle: int32 [24, 48, 128], P('stream', 'span'), may hold values from 0 to 1, as said below
- block_level: int32 [4, 8], replicated, may hold values 0 or 1
- relax_rates: float32 [27], replicated, may hold values from 0.5 to 1.9
Outputs:
- fine_next: float32 [27, 24, 48, 128], P(None, 'stream', 'span')
- coarse_next: float32 [27, 12, 24, 64], P(None, 'stream', 'span')
Inputs may be any that keep to these rules, and one draw needn't show every extreme that they name: `block_level`: 1 marks a refined block, whose fine cells are active; 0 a coarse block. `obstacle`: 1 marks a building cell. No building cell has a first index x with x % 6 below 2 or at least 4, nor a second index y with y % 6 below 2 or at least 4; a building cell stands on the ground or on another building cell.
All inputs are finite; a program needn't handle non-finite values.
Results may differ from a plain program's by a relative error of at most 0.0003.
Values sent between devices are 32-bit elements; how exact they have to be, the bound alone decides.
No kernel may reach another device: no remote copies, remote signals or barrier semaphores. Data moves between devices by JAX's collectives and lax.ppermute only.
A program may use at most 64 MiB of HBM per device.

v0:
```python
import jax
import jax.numpy as jnp
from jax import lax
from jax.experimental import pallas as pl
from jax.experimental.pallas import tpu as pltpu
from jax.sharding import PartitionSpec as P

F32 = jnp.float32
Q = 27
LANES = 128
OCTETS = [(8 * o, min(8, Q - 8 * o)) for o in range(4)]
STEP = [(q // 9 - 1, q // 3 % 3 - 1, q % 3 - 1) for q in range(Q)]
HIGH_X = [q for q in range(Q) if STEP[q][0] == 1]
LOW_X = [q for q in range(Q) if STEP[q][0] == -1]
HIGH_Y = [q for q in range(Q) if STEP[q][1] == 1]
LOW_Y = [q for q in range(Q) if STEP[q][1] == -1]

VMEM = pl.BlockSpec(memory_space=pltpu.VMEM)
SMEM = pl.BlockSpec(memory_space=pltpu.SMEM)
ANY = pl.BlockSpec(memory_space=pl.ANY)
LIMIT = 16 << 20


def params(**more):
    return pltpu.CompilerParams(vmem_limit_bytes=LIMIT, **more)


def struct(shape, dtype=F32):
    return jax.ShapeDtypeStruct(shape, dtype)


def ring(axis, by):
    peers = lax.axis_size(axis)
    return [(i, (i + by) % peers) for i in range(peers)]


X_SECOND, X_FINE = 32, 48
Y_FINE = 72


def roll_lane(v, by):
    return v if by == 0 else pltpu.roll(v, by % v.shape[1], 1)


def roll_sub(v, by):
    return v if by == 0 else pltpu.roll(v, by % v.shape[0], 0)


def lane_iota():
    return lax.broadcasted_iota(jnp.int32, (8, LANES), 1)


def sub_iota():
    return lax.broadcasted_iota(jnp.int32, (8, LANES), 0)


def take(v, idx, axis):
    return jnp.take_along_axis(v, idx, axis=axis)


def pack_x_kernel(sx, fine, coarse, up, down, f_low, f_high, c_low, c_high, sems):
    cx = sx // 2
    copies = [
        pltpu.make_async_copy(fine.at[sx - 1], f_high, sems.at[0]),
        pltpu.make_async_copy(coarse.at[cx - 1], c_high, sems.at[1]),
        pltpu.make_async_copy(fine.at[0], f_low, sems.at[2]),
        pltpu.make_async_copy(coarse.at[0], c_low, sems.at[3]),
    ]
    for c in copies:
        c.start()
    sy = f_low.shape[0]
    nzc = c_low.shape[2]
    for k, (out, f, c, qs) in enumerate(((up, f_high, c_high, HIGH_X), (down, f_low, c_low, LOW_X))):
        copies[2 * k].wait()
        copies[2 * k + 1].wait()
        out[0:Q, 0:nzc] = c[0]
        out[0:Q, nzc : 2 * nzc] = c[1]
        out[X_SECOND : X_SECOND + 16, 0:nzc] = c[2, 0:16]
        out[X_SECOND : X_SECOND + Q - 16, nzc : 2 * nzc] = c[2, 16:Q]
        for y in range(sy):
            out[X_FINE + 9 * y : X_FINE + 9 * y + 9] = f[y, qs[0] : qs[0] + 9]


def fine_plane(fine, from_low, from_high, y):
    sx = fine.shape[0]
    base = X_FINE + 9 * y
    rows = [None] * Q
    for q0, n in OCTETS:
        cells = [fine[x, y, q0 : q0 + n] for x in range(sx)]
        low, high = (cells[0], cells[0])
        if q0 == 16:
            low = from_low[base - 2 : base + 6]
        if q0 == 24:
            low = from_low[base + 6 : base + 9]
        if q0 == 0:
            high = from_high[base : base + 8]
        if q0 == 8:
            high = jnp.broadcast_to(from_high[base + 8 : base + 9], (8, LANES))
        tile = jnp.swapaxes(jnp.stack([low, *cells, high]), 0, 1)
        for k in range(n):
            rows[q0 + k] = tile[k]
    return rows


def coarse_ghost(msg, Y, q0, n, nzc):
    if Y == 0:
        return msg[q0 : q0 + n, 0:nzc]
    if Y == 1:
        return roll_lane(msg[q0 : q0 + n], nzc)[:, 0:nzc]
    if q0 < 16:
        return msg[X_SECOND + q0 : X_SECOND + q0 + n, 0:nzc]
    return roll_lane(msg[X_SECOND + q0 - 16 : X_SECOND + q0 - 16 + n], nzc)[:, 0:nzc]


def coarse_plane(coarse, from_low, from_high, Y):
    cx, nzc = coarse.shape[0], coarse.shape[3]
    rows = [None] * Q
    for q0, n in OCTETS:
        cells = [coarse[X, Y, q0 : q0 + n] for X in range(cx)]
        low = coarse_ghost(from_low, Y, q0, n, nzc)
        high = coarse_ghost(from_high, Y, q0, n, nzc)
        fill = [high] * (8 - cx - 2)
        tile = jnp.swapaxes(jnp.stack([low, *cells, high, *fill]), 0, 1)
        for k in range(n):
            rows[q0 + k] = tile[k]
    return rows


def pack_y_kernel(fine, coarse, from_low, from_high, up, down, w_edge, c_all):
    sy, cy, nzc = fine.shape[1], coarse.shape[1], coarse.shape[3]
    for Y in range(cy):
        for q, v in enumerate(coarse_plane(coarse, from_low, from_high, Y)):
            c_all[q, Y, :, 0:nzc] = v
    low_half = lane_iota() < nzc
    for out, e, y, Y, qs in ((up, 1, sy - 1, cy - 1, HIGH_Y), (down, 0, 0, 0, LOW_Y)):
        for p in range((Q + 1) // 2):
            a = c_all[2 * p, Y]
            if 2 * p + 1 < Q:
                a = jnp.where(low_half, a, roll_lane(c_all[2 * p + 1, Y], nzc))
            out[5 * p : 5 * p + 5] = a[0:5]
        rows = fine_plane(fine, from_low, from_high, y)
        for q in range(Q):
            w_edge[q, e] = rows[q]
        for k, q in enumerate(qs):
            out[Y_FINE + 8 * k : Y_FINE + 8 * k + 8] = rows[q]


def explode_tables(nzc):
    lane, sub = lane_iota(), sub_iota()
    za = lane >> 1
    zb = jnp.clip(za + jnp.where((lane & 1) == 1, 1, -1), 0, nzc - 1)
    x = sub + 1
    xa = x >> 1
    xb = xa + jnp.where((x & 1) == 1, 1, -1)
    return za, zb, xa, xb


def explode_zx(v, tables):
    za, zb, xa, xb = tables
    t = 0.75 * take(v, za, 1) + 0.25 * take(v, zb, 1)
    return 0.75 * take(t, xa, 0) + 0.25 * take(t, xb, 0)


def y_pair(j):
    a = (j + 1) >> 1
    return a, a + (1 if (j + 1) & 1 else -1)


def explode_y(ex, j):
    a, b = y_pair(j)
    return 0.75 * ex[a] + 0.25 * ex[b]


def forward(m0, m1, m2):
    pair = m0 + m2
    return pair + 4.0 * m1, m2 - m0, pair


def collide(g, keep, gain):
    t = [None] * Q
    for r in range(9):
        t[r], t[9 + r], t[18 + r] = forward(g[r], g[9 + r], g[18 + r])
    cols = [(t[c] + t[6 + c]) + 4.0 * t[3 + c] for c in range(3)]
    density = (cols[0] + cols[2]) + 4.0 * cols[1]
    inv = 1.0 / density
    rows = [(t[3 * b] + t[3 * b + 2]) + 4.0 * t[3 * b + 1] for b in (0, 2)]
    uy = (rows[1] - rows[0]) * inv
    uz = (cols[2] - cols[0]) * inv
    dcols = [(t[9 + c] + t[15 + c]) + 4.0 * t[12 + c] for c in range(3)]
    ux = ((dcols[0] + dcols[2]) + 4.0 * dcols[1]) * inv
    for r in range(9):
        t0, d, pair = t[r], t[9 + r], t[18 + r]
        t1 = d - ux * t0
        t[9 + r], t[18 + r] = t1, pair - ux * (d + t1)
    for u, lines in ((uy, [(9 * a + c, 3) for a in range(3) for c in range(3)]),
                     (uz, [(9 * a + 3 * b, 1) for a in range(3) for b in range(3)])):
        for at, by in lines:
            t0, d, pair = forward(t[at], t[at + by], t[at + 2 * by])
            t1 = d - u * t0
            t[at], t[at + by], t[at + 2 * by] = t0, t1, pair - u * (d + t1)
    for q in range(Q):
        t[q] = keep[q] * t[q]
        if q in gain:
            t[q] = t[q] + gain[q] * density
    for u, lines in ((uz, [(9 * a + 3 * b, 1) for a in range(3) for b in range(3)]),
                     (uy, [(9 * a + c, 3) for a in range(3) for c in range(3)]),
                     (ux, [(r, 9) for r in range(9)])):
        for at, by in lines:
            t0, t1, t2 = t[at], t[at + by], t[at + 2 * by]
            d = t1 + u * t0
            s = t2 + u * (t1 + d)
            t[at], t[at + by], t[at + 2 * by] = s - d, 0.5 * (t0 - s), s + d
    return t


EVEN = [9 * a + 3 * b + c for a in (0, 2) for b in (0, 2) for c in (0, 2)]


def gain_of(q):
    return (1.0 if q // 9 == 0 else 1.0 / 3.0) * (1.0 if q // 3 % 3 == 0 else 1.0 / 3.0) * (
        1.0 if q % 3 == 0 else 1.0 / 3.0)


def pull(source, center, step_mask):
    out = []
    for q in range(Q):
        ex, ey, ez = STEP[q]
        v = roll_lane(roll_sub(source(q), ex), ez)
        mask = step_mask(ex, ey, ez)
        if mask is not None:
            v = jnp.where(mask, center(26 - q), v)
        out.append(v)
    return out


def edge_masks(height):
    lane = lane_iota()
    return {1: lane == 0, -1: lane == height - 1}


def fine_mask(y, first_wall, flags, edges):
    def mask_of(ex, ey, ez):
        m = None
        if (ex, ey, ez) == (0, 0, 0):
            return None
        s = y - ey - first_wall
        if s in (0, 1):
            m = roll_lane(roll_sub(flags[s], ex), ez) == 1
        if ez != 0:
            m = edges[ez] if m is None else m | edges[ez]
        return m

    return mask_of


def store_rows(rows, out, y, xs, width):
    for q0, n in OCTETS:
        tile = jnp.swapaxes(jnp.stack(rows[q0 : q0 + n]), 0, 1)
        for k, x in enumerate(xs):
            out[k, y, q0 : q0 + n] = tile[x][:, 0:width]


def coalesce(first, second, index):
    rows = []
    for a, b in zip(first, second):
        s = a + b
        s = s + roll_sub(s, -1)
        s = s + roll_lane(s, -1)
        rows.append(0.125 * take(s, index, 1))
    return rows


def inner_kernel(fine, coarse, from_low, from_high, c_all, obstacle, level, rates,
                 out, c_out, w_in, ex_in, coef, levels, flag_out, c_wall, f_buf, c_buf, sems):
    sx, sy, nz = fine.shape[0], fine.shape[1], fine.shape[3]
    cx, cy, nzc = coarse.shape[0], coarse.shape[1], coarse.shape[3]
    row, col = lax.axis_index("stream"), lax.axis_index("span")
    n_row, n_col = level.shape
    own = level[row, col]
    lane, sub = lane_iota(), sub_iota()
    at_row = [lax.rem(row + n_row - 1, n_row), row, lax.rem(row + 1, n_row)]
    at_col = [lax.rem(col + n_col - 1, n_col), col, lax.rem(col + 1, n_col)]
    for k in range(3):
        v = jnp.where(sub == 0, level[at_row[0], at_col[k]],
                      jnp.where(sub == sx + 1, level[at_row[2], at_col[k]], level[at_row[1], at_col[k]]))
        levels[k] = v
    refined_block = jnp.full((8, LANES), own, jnp.int32) == 1
    keep, gain = {}, {}
    for q in range(Q):
        s = jnp.full((8, LANES), rates[q], F32)
        s = jnp.where(refined_block, s, 1.0 / (2.0 / s - 0.5))
        keep[q] = 0.125 - 0.125 * s
        coef[q] = keep[q]
        if q in EVEN:
            gain[q] = (0.125 * gain_of(q)) * s
            coef[Q + EVEN.index(q)] = gain[q]
    tables = explode_tables(nzc)
    for Y in range(cy):
        for q in range(Q):
            ex_in[q, Y] = explode_zx(c_all[q, Y], tables)
    mid = sy // 2
    flags = []
    for y in (mid - 1, mid):
        v = jnp.zeros((8, LANES), jnp.int32)
        for x in (sx // 2 - 1, sx // 2):
            v = jnp.where(sub == x + 1, jnp.broadcast_to(obstacle[x, y : y + 1, :], (8, LANES)), v)
        flags.append(v)
        flag_out[len(flags) - 1] = v
    both = jnp.maximum(flags[0], flags[1])
    both = jnp.maximum(both, roll_sub(both, -1))
    both = jnp.maximum(both, roll_lane(both, -1))
    half = (2 * lane) & (LANES - 1)
    both = take(both, half, 1)
    both = jnp.broadcast_to(both[sx // 2 : sx // 2 + 1], (8, LANES))
    wall = jnp.where((sub == 1 + cx // 2) & (lane < nzc), both, 0)
    c_wall[...] = wall
    edges = edge_masks(nz)

    @pl.when(own == 1)
    def _():
        near = levels[1] == 1
        for y in range(1, sy - 1):
            rows = fine_plane(fine, from_low, from_high, y)
            for q in range(Q):
                v = rows[q]
                if STEP[q][0] != 0:
                    a, b = y_pair(y + 1)
                    v = jnp.where(near, v, 0.75 * ex_in[q, a - 1] + 0.25 * ex_in[q, b - 1])
                w_in[q, y - 1] = v
        results = []
        for t, y in enumerate((mid - 1, mid)):
            pulled = pull(lambda q: w_in[q, y - 1 - STEP[q][1]], lambda q: w_in[q, y - 1],
                          fine_mask(y, mid - 1, flags, edges))
            new = collide(pulled, coef, {q: coef[Q + k] for k, q in enumerate(EVEN)})
            stay = flags[t] == 1
            new = [jnp.where(stay, w_in[q, y - 1], new[q]) for q in range(Q)]
            store_rows(new, f_buf, t, range(1, sx + 1), nz)
            results.append(new)
        store_rows(coalesce(results[0], results[1], half), c_buf, 0, range(1, sx + 1, 2), nzc)

    @pl.when(own != 1)
    def _():
        for t, y in enumerate((mid - 1, mid)):
            a, b = y_pair(y + 1)
            rows = [0.75 * ex_in[q, a - 1] + 0.25 * ex_in[q, b - 1] for q in range(Q)]
            store_rows(rows, f_buf, t, range(1, sx + 1), nz)
        Y = cy // 2
        coarse_pull(lambda q, J: c_all[q, J - 1], Y + 1, wall, coef, c_buf, 0, nzc, cx, 1 + cy // 2)

    copies = [pltpu.make_async_copy(f_buf, out.at[:, pl.ds(mid - 1, 2)], sems.at[0]),
              pltpu.make_async_copy(c_buf, c_out.at[:, pl.ds(cy // 2, 1)], sems.at[1])]
    for c in copies:
        c.start()
    for c in copies:
        c.wait()


def coarse_pull(plane, J, wall, coef, buf, at, nzc, cx, wall_row):
    edges = edge_masks(nzc)

    def mask_of(ex, ey, ez):
        m = None
        if (ex, ey, ez) == (0, 0, 0):
            return None
        if J - ey == wall_row:
            m = roll_lane(roll_sub(wall, ex), ez) == 1
        if ez != 0:
            m = edges[ez] if m is None else m | edges[ez]
        return m

    pulled = pull(lambda q: plane(q, J - STEP[q][1]), lambda q: plane(q, J), mask_of)
    new = collide(pulled, coef, {q: coef[Q + k] for k, q in enumerate(EVEN)})
    if J == wall_row:
        stay = wall == 1
        new = [jnp.where(stay, plane(q, J), new[q]) for q in range(Q)]
    store_rows(new, buf, at, range(1, cx + 1), nzc)


def outer_kernel(from_below, from_above, w_edge, w_in, c_all, ex_in, coef, levels, flags, c_wall, level,
                 _out_in, _c_in, out, c_out, ex_g, c_g, w_g, w_e, f_low, f_high, c_low, c_high, sems):
    sx, sy, nz = out.shape[0], out.shape[1], out.shape[3]
    cx, cy, nzc = c_out.shape[0], c_out.shape[1], c_out.shape[3]
    own = level[lax.axis_index("stream"), lax.axis_index("span")]
    lane = lane_iota()
    tables = explode_tables(nzc)
    for e, msg in enumerate((from_below, from_above)):
        for p in range((Q + 1) // 2):
            v = msg[5 * p : 5 * p + 8]
            c_g[2 * p, e] = v
            ex_g[2 * p, e] = explode_zx(v, tables)
            if 2 * p + 1 < Q:
                v = roll_lane(v, nzc)
                c_g[2 * p + 1, e] = v
                ex_g[2 * p + 1, e] = explode_zx(v, tables)

    def exploded(q, J):
        if J == 0:
            return ex_g[q, 0]
        if J == cy + 1:
            return ex_g[q, 1]
        return ex_in[q, J - 1]

    def explode_at(q, j):
        a, b = y_pair(j)
        return 0.75 * exploded(q, a) + 0.25 * exploded(q, b)

    half = (2 * lane) & (LANES - 1)
    edges = edge_masks(nz)
    parts = ((0, f_low, c_low, (0, 1)), (1, f_high, c_high, (sy - 2, sy - 1)))

    def copies(e):
        _, f_buf, c_buf, ys = parts[e]
        return (pltpu.make_async_copy(f_buf, out.at[:, pl.ds(ys[0], 2)], sems.at[2 * e]),
                pltpu.make_async_copy(c_buf, c_out.at[:, pl.ds((cy - 1) * e, 1)], sems.at[2 * e + 1]))

    @pl.when(own == 1)
    def _():
        for e, f_buf, c_buf, ys in parts:
            msg = from_below if e == 0 else from_above
            ghost_j = 0 if e == 0 else sy + 1
            edge_j = 1 if e == 0 else sy
            far = levels[0 if e == 0 else 2] == 1
            near = levels[1] == 1
            qs = HIGH_Y if e == 0 else LOW_Y
            for k, q in enumerate(qs):
                w_g[k] = jnp.where(far, msg[Y_FINE + 8 * k : Y_FINE + 8 * k + 8], explode_at(q, ghost_j))
            for q in range(Q):
                if STEP[q][0] != 0:
                    w_e[q, e] = jnp.where(near, w_edge[q, e], explode_at(q, edge_j))
                else:
                    w_e[q, e] = w_edge[q, e]

            def plane(q, j):
                if j == ghost_j:
                    return w_g[qs.index(q)]
                if j == edge_j:
                    return w_e[q, e]
                return w_in[q, j - 2]

            results = []
            for t, y in enumerate(ys):
                pulled = pull(lambda q: plane(q, y + 1 - STEP[q][1]), lambda q: plane(q, y + 1),
                              fine_mask(y, sy // 2 - 1, flags, edges))
                new = collide(pulled, coef, {q: coef[Q + k] for k, q in enumerate(EVEN)})
                store_rows(new, f_buf, t, range(1, sx + 1), nz)
                results.append(new)
            store_rows(coalesce(results[0], results[1], half), c_buf, 0, range(1, sx + 1, 2), nzc)
            for c in copies(e):
                c.start()

    @pl.when(own != 1)
    def _():
        wall = c_wall[...]

        def plane(q, J):
            if J == 0:
                return c_g[q, 0]
            if J == cy + 1:
                return c_g[q, 1]
            return c_all[q, J - 1]

        for e, f_buf, c_buf, ys in parts:
            for t, y in enumerate(ys):
                store_rows([explode_at(q, y + 1) for q in range(Q)], f_buf, t, range(1, sx + 1), nz)
            J = 1 if e == 0 else cy
            coarse_pull(plane, J, wall, coef, c_buf, 0, nzc, cx, 1 + cy // 2)
            for c in copies(e):
                c.start()

    for e in range(2):
        for c in copies(e):
            c.wait()


def cost(flops, nbytes):
    return pl.CostEstimate(flops=flops, bytes_accessed=nbytes, transcendentals=0)


def local(fine_pops, coarse_pops, obstacle, block_level, relax_rates):
    fine = jnp.transpose(fine_pops, (1, 2, 0, 3))
    coarse = jnp.transpose(coarse_pops, (1, 2, 0, 3))
    sx, sy, _, nz = fine.shape
    cx, cy, _, nzc = coarse.shape

    x_rows = X_FINE + 8 * ((9 * sy + 7) // 8)
    x_message = struct((x_rows, LANES))
    up, down = pl.pallas_call(
        lambda *refs: pack_x_kernel(sx, *refs),
        out_shape=(x_message, x_message),
        in_specs=[ANY, ANY],
        out_specs=(VMEM, VMEM),
        scratch_shapes=[
            pltpu.VMEM((sy, Q, nz), F32),
            pltpu.VMEM((sy, Q, nz), F32),
            pltpu.VMEM((cy, Q, nzc), F32),
            pltpu.VMEM((cy, Q, nzc), F32),
            pltpu.SemaphoreType.DMA((4,)),
        ],
        compiler_params=params(),
        name="pack_x",
    )(fine, coarse)
    from_low = lax.ppermute(up, "stream", ring("stream", 1))
    from_high = lax.ppermute(down, "stream", ring("stream", -1))

    y_message = struct((Y_FINE + 72, LANES))
    up, down, w_edge, c_all = pl.pallas_call(
        pack_y_kernel,
        out_shape=(y_message, y_message, struct((Q, 2, 8, LANES)), struct((Q, cy, 8, LANES))),
        in_specs=[VMEM] * 4,
        out_specs=(VMEM,) * 4,
        compiler_params=params(),
        name="pack_y",
    )(fine, coarse, from_low, from_high)
    from_below = lax.ppermute(up, "span", ring("span", 1))
    from_above = lax.ppermute(down, "span", ring("span", -1))

    fine_shape, coarse_shape = struct(fine.shape), struct(coarse.shape)
    out, c_out, w_in, ex_in, coef, levels, flags, c_wall = pl.pallas_call(
        inner_kernel,
        out_shape=(
            fine_shape,
            coarse_shape,
            struct((Q, sy - 2, 8, LANES)),
            struct((Q, cy, 8, LANES)),
            struct((Q + len(EVEN), 8, LANES)),
            struct((3, 8, LANES), jnp.int32),
            struct((2, 8, LANES), jnp.int32),
            struct((8, LANES), jnp.int32),
        ),
        in_specs=[VMEM] * 6 + [SMEM] * 2,
        out_specs=(ANY, ANY) + (VMEM,) * 6,
        scratch_shapes=[
            pltpu.VMEM((sx, 2, Q, nz), F32),
            pltpu.VMEM((cx, 1, Q, nzc), F32),
            pltpu.SemaphoreType.DMA((2,)),
        ],
        compiler_params=params(),
        cost_estimate=cost(20_000_000, 1_000_000),
        name="inner",
    )(fine, coarse, from_low, from_high, c_all, obstacle, block_level, relax_rates)

    out, c_out = pl.pallas_call(
        outer_kernel,
        out_shape=(fine_shape, coarse_shape),
        in_specs=[VMEM] * 10 + [SMEM, ANY, ANY],
        out_specs=(ANY, ANY),
        scratch_shapes=[
            pltpu.VMEM((Q, 2, 8, LANES), F32),
            pltpu.VMEM((Q, 2, 8, LANES), F32),
            pltpu.VMEM((9, 8, LANES), F32),
            pltpu.VMEM((Q, 2, 8, LANES), F32),
            pltpu.VMEM((sx, 2, Q, nz), F32),
            pltpu.VMEM((sx, 2, Q, nz), F32),
            pltpu.VMEM((cx, 1, Q, nzc), F32),
            pltpu.VMEM((cx, 1, Q, nzc), F32),
            pltpu.SemaphoreType.DMA((4,)),
        ],
        input_output_aliases={11: 0, 12: 1},
        compiler_params=params(),
        name="outer",
    )(from_below, from_above, w_edge, w_in, c_all, ex_in, coef, levels, flags, c_wall, block_level,
      out, c_out)
    return jnp.transpose(out, (2, 0, 1, 3)), jnp.transpose(c_out, (2, 0, 1, 3))


def solution(mesh):
    placed = (
        P(None, "stream", "span", None),
        P(None, "stream", "span", None),
        P("stream", "span", None),
        P(),
        P(),
    )
    return jax.shard_map(
        local,
        mesh=mesh,
        in_specs=placed,
        out_specs=(P(None, "stream", "span", None), P(None, "stream", "span", None)),
        check_vma=False,
    )
```

profile of v0, /device:TPU:3, one launch (start us, length us, event | category | flops | bytes accessed | tf_op | source)
XLA Modules:
  0.0 19.0 jit_solution(11956392206167232199)
XLA Ops:
  0.6 0.0 copy-start
  0.6 1.1 %copy-done = f32[27,6,6,128]{3,0,2,1:T(8,128)S(1)} copy-done((f32[27,6,6,128]{3,0,2,1:T(8,128)S(1)}, f32[27,6,6,128]{3,0,2,1:T(8,128)}, u32[]{:S(2)}) %copy-start) | copy-done | bytes 497688
  1.7 0.0 copy-start.1
  1.7 0.9 %copy-done.1 = f32[27,3,3,64]{3,0,2,1:T(8,128)S(1)} copy-done((f32[27,3,3,64]{3,0,2,1:T(8,128)S(1)}, f32[27,3,3,64]{3,0,2,1:T(8,128)}, u32[]{:S(2)}) %copy-start.1) | copy-done | bytes 62232
  2.6 0.3 %pack_x.1 = (f32[104,128]{1,0:T(8,128)S(1)}, f32[104,128]{1,0:T(8,128)S(1)}) custom-call(f32[6,6,27,128]{3,2,1,0:T(8,128)S(1)} %bitcast.4, f32[3,3,27,64]{3,2,1,0:T(8,128)S(1)} %bitcast.7), custom_call_target="tpu_custom_call" | custom-call | tf_op jit(solution)/shard_map/pack_x/pallas_call | solution.py:487
  2.9 1.3 %collective-permute-start = (f32[104,128]{1,0:T(8,128)S(1)}, f32[104,128]{1,0:T(8,128)S(1)}, u32[]{:S(2)}, u32[]{:S(2)}) collective-permute-start(f32[104,128]{1,0:T(8,128)S(1)} %get-tuple-element.18), channel_id=1, source_target_pairs={{0,8},{8,16},{16,24},{24,0},{1,9},{9,17},{17,25},{25,1},{2,10},{10... | collective-permute-start | bytes 159752 | tf_op jit(solution)/shard_map/ppermute | solution.py:502
  4.1 0.0 copy-start.2
  4.1 0.3 %collective-permute-start.1 = (f32[104,128]{1,0:T(8,128)S(1)}, f32[104,128]{1,0:T(8,128)S(1)}, u32[]{:S(2)}, u32[]{:S(2)}) collective-permute-start(f32[104,128]{1,0:T(8,128)S(1)} %get-tuple-element.19), channel_id=1, source_target_pairs={{0,24},{8,0},{16,8},{24,16},{1,25},{9,1},{17,9},{25,17},{2,26},{10... | collective-permute-start | bytes 159752 | tf_op jit(solution)/shard_map/ppermute | solution.py:503
  4.4 1.5 %collective-permute-done.from_low = f32[104,128]{1,0:T(8,128)S(1)} collective-permute-done((f32[104,128]{1,0:T(8,128)S(1)}, f32[104,128]{1,0:T(8,128)S(1)}, u32[]{:S(2)}, u32[]{:S(2)}) %collective-permute-start) | collective-permute-done | bytes 53280 | tf_op jit(solution)/shard_map/ppermute | solution.py:502
  5.9 2.7 %collective-permute-done.1.from_high = f32[104,128]{1,0:T(8,128)S(1)} collective-permute-done((f32[104,128]{1,0:T(8,128)S(1)}, f32[104,128]{1,0:T(8,128)S(1)}, u32[]{:S(2)}, u32[]{:S(2)}) %collective-permute-start.1) | collective-permute-done | bytes 53280 | tf_op jit(solution)/shard_map/ppermute | solution.py:503
  8.6 0.2 pack_y.1
  8.7 0.0 copy-start.3
  8.7 2.8 %collective-permute-start.2 = (f32[144,128]{1,0:T(8,128)S(1)}, f32[144,128]{1,0:T(8,128)S(1)}, u32[]{:S(2)}, u32[]{:S(2)}) collective-permute-start(f32[144,128]{1,0:T(8,128)S(1)} %get-tuple-element.20), channel_id=1, source_target_pairs={{0,1},{1,2},{2,3},{3,4},{4,5},{5,6},{6,7},{7,0},{8,9},{9,10},{10,1... | collective-permute-start | bytes 221192 | tf_op jit(solution)/shard_map/ppermute | solution.py:514
  11.5 0.0 copy-start.4
  11.5 0.0 collective-permute-start.3
  11.5 0.0 copy-done.2
  11.5 0.0 copy-done.3
  11.5 0.6 %copy-done.4 = f32[27]{0:T(128)S(1)} copy-done((f32[27]{0:T(128)S(1)}, f32[27]{0:T(128)}, u32[]{:S(2)}) %copy-start.4) | copy-done | bytes 132
  12.2 2.1 %inner.1 = (f32[6,6,27,128]{3,2,1,0:T(8,128)}, f32[3,3,27,64]{3,2,1,0:T(8,128)}, f32[27,4,8,128]{3,2,1,0:T(8,128)S(1)}, f32[27,3,8,128]{3,2,1,0:T(8,128)S(1)}, f...) custom-call(f32[6,6,27,128]{3,2,1,0:T(8,128)S(1)} %bitcast.6, ...), custom_call_target="tpu_custom_call" | custom-call | flops 20000000 | bytes 1000000 | tf_op jit(solution)/shard_map/inner/pallas_call | solution.py:518
  14.3 0.0 collective-permute-done.2.from_below
  14.3 1.7 %collective-permute-done.3.from_above = f32[144,128]{1,0:T(8,128)S(1)} collective-permute-done((f32[144,128]{1,0:T(8,128)S(1)}, f32[144,128]{1,0:T(8,128)S(1)}, u32[]{:S(2)}, u32[]{:S(2)}) %collective-permute-start.3) | collective-permute-done | bytes 73760 | tf_op jit(solution)/shard_map/ppermute | solution.py:515
  16.0 3.0 %outer.1 = (f32[6,6,27,128]{3,2,1,0:T(8,128)}, f32[3,3,27,64]{3,2,1,0:T(8,128)}) custom-call(f32[144,128]{1,0:T(8,128)S(1)} %collective-permute-done.2.from_below, f32[144,128]{1,0:T(8,128)S(1)} %collective-permute-done.3.from_above, f32[27,2,8,128]{3,2,1,0:T(8,128)S(1)} %get-tuple-element.22.w_edge, ...), custom_call_target="tpu_custom_call", output_to_operand_aliasing={{0}: (11, {}), {1}: (12, {})} | custom-call | tf_op jit(solution)/shard_map/outer/pallas_call | solution.py:542
Async XLA Ops:
  0.6 1.1 %copy-start = (f32[27,6,6,128]{3,0,2,1:T(8,128)S(1)}, f32[27,6,6,128]{3,0,2,1:T(8,128)}, u32[]{:S(2)}) copy-start(f32[27,6,6,128]{3,0,2,1:T(8,128)} %param.5) | copy-start | bytes 1492996
  1.7 0.9 %copy-start.1 = (f32[27,3,3,64]{3,0,2,1:T(8,128)S(1)}, f32[27,3,3,64]{3,0,2,1:T(8,128)}, u32[]{:S(2)}) copy-start(f32[27,3,3,64]{3,0,2,1:T(8,128)} %param.6) | copy-start | bytes 186628
  2.9 3.0 %collective-permute-start = (f32[104,128]{1,0:T(8,128)S(1)}, f32[104,128]{1,0:T(8,128)S(1)}, u32[]{:S(2)}, u32[]{:S(2)}) collective-permute-start(f32[104,128]{1,0:T(8,128)S(1)} %get-tuple-element.18), channel_id=1, source_target_pairs={{0,8},{8,16},{16,24},{24,0},{1,9},{9,17},{17,25},{25,1},{2,10},{10... | collective-permute-start | bytes 159752 | tf_op jit(solution)/shard_map/ppermute | solution.py:502
  4.1 7.4 %copy-start.2 = (s32[6,6,128]{2,1,0:T(8,128)S(1)}, s32[6,6,128]{2,1,0:T(8,128)}, u32[]{:S(2)}) copy-start(s32[6,6,128]{2,1,0:T(8,128)} %obstacle.1) | copy-start | bytes 55300
  4.1 4.4 %collective-permute-start.1 = (f32[104,128]{1,0:T(8,128)S(1)}, f32[104,128]{1,0:T(8,128)S(1)}, u32[]{:S(2)}, u32[]{:S(2)}) collective-permute-start(f32[104,128]{1,0:T(8,128)S(1)} %get-tuple-element.19), channel_id=1, source_target_pairs={{0,24},{8,0},{16,8},{24,16},{1,25},{9,1},{17,9},{25,17},{2,26},{10... | collective-permute-start | bytes 159752 | tf_op jit(solution)/shard_map/ppermute | solution.py:503
  8.7 2.8 %copy-start.3 = (s32[4,8]{1,0:T(4,128)S(1)}, s32[4,8]{1,0:T(4,128)}, u32[]{:S(2)}) copy-start(s32[4,8]{1,0:T(4,128)} %level.3) | copy-start | bytes 388
  8.7 5.5 %collective-permute-start.2 = (f32[144,128]{1,0:T(8,128)S(1)}, f32[144,128]{1,0:T(8,128)S(1)}, u32[]{:S(2)}, u32[]{:S(2)}) collective-permute-start(f32[144,128]{1,0:T(8,128)S(1)} %get-tuple-element.20), channel_id=1, source_target_pairs={{0,1},{1,2},{2,3},{3,4},{4,5},{5,6},{6,7},{7,0},{8,9},{9,10},{10,1... | collective-permute-start | bytes 221192 | tf_op jit(solution)/shard_map/ppermute | solution.py:514
  11.5 0.7 %copy-start.4 = (f32[27]{0:T(128)S(1)}, f32[27]{0:T(128)}, u32[]{:S(2)}) copy-start(f32[27]{0:T(128)} %rates.1) | copy-start | bytes 328
  11.5 4.5 %collective-permute-start.3 = (f32[144,128]{1,0:T(8,128)S(1)}, f32[144,128]{1,0:T(8,128)S(1)}, u32[]{:S(2)}, u32[]{:S(2)}) collective-permute-start(f32[144,128]{1,0:T(8,128)S(1)} %get-tuple-element.21), channel_id=1, source_target_pairs={{0,7},{1,0},{2,1},{3,2},{4,3},{5,4},{6,5},{7,6},{8,15},{9,8},{10,9... | collective-permute-start | bytes 221192 | tf_op jit(solution)/shard_map/ppermute | solution.py:515
where the time goes:
time: 19.2 us; the launch traced here: 19 us
  waiting for transfers between devices  5.93 us (31%)
  Pallas kernels  5.46 us (28%)
  starting transfers between devices  4.31 us (22%)
  local copies, waits for them, and re-layouts  2.62 us (14%)
  between operations  0.67 us (3%)
    pallas_call x1, Pallas kernels, local(): pl.pallas_call(outer_kernel, out_shape=(fine_shape, coarse_shape), in_spe...  2.96 us
    ppermute x1, starting transfers between devices, local(): from_below = lax.ppermute(up, 'span', ring('span', 1))  2.79 us
    ppermute x1, waiting for transfers between devices, local(): from_high = lax.ppermute(down, 'stream', ring('stream', -1))  2.66 us
    unnamed x10, local copies, waits for them, and re-layouts  2.62 us
    pallas_call x1, Pallas kernels, local(): pl.pallas_call(inner_kernel, out_shape=(fine_shape, coarse_shape, struct(...  2.07 us
    ppermute x1, waiting for transfers between devices, local(): from_above = lax.ppermute(down, 'span', ring('span', -1))  1.75 us
    ppermute x1, waiting for transfers between devices, local(): from_low = lax.ppermute(up, 'stream', ring('stream', 1))  1.52 us
    ppermute x1, starting transfers between devices, local(): from_low = lax.ppermute(up, 'stream', ring('stream', 1))  1.26 us
  transfers between devices with their start and end apart: 4, of which 3 were waited for; matrix products, arithmetic and copies ran while one was open for 0% of the time, Pallas kernels for 11%

commit v1 on v0

--- a/solution.py
+++ b/solution.py
@@ -18,6 +18,7 @@
 VMEM = pl.BlockSpec(memory_space=pltpu.VMEM)
 SMEM = pl.BlockSpec(memory_space=pltpu.SMEM)
 ANY = pl.BlockSpec(memory_space=pl.ANY)
+HBM = pl.BlockSpec(memory_space=pltpu.HBM)
 LIMIT = 16 << 20
 
 
@@ -476,6 +477,10 @@
     return pl.CostEstimate(flops=flops, bytes_accessed=nbytes, transcendentals=0)
 
 
+def in_hbm(x):
+    return pltpu.with_memory_space_constraint(x, pltpu.HBM)
+
+
 def local(fine_pops, coarse_pops, obstacle, block_level, relax_rates):
     fine = jnp.transpose(fine_pops, (1, 2, 0, 3))
     coarse = jnp.transpose(coarse_pops, (1, 2, 0, 3))
@@ -487,7 +492,7 @@
     up, down = pl.pallas_call(
         lambda *refs: pack_x_kernel(sx, *refs),
         out_shape=(x_message, x_message),
-        in_specs=[ANY, ANY],
+        in_specs=[HBM, HBM],
         out_specs=(VMEM, VMEM),
         scratch_shapes=[
             pltpu.VMEM((sy, Q, nz), F32),
@@ -498,7 +503,7 @@
         ],
         compiler_params=params(),
         name="pack_x",
-    )(fine, coarse)
+    )(in_hbm(fine), in_hbm(coarse))
     from_low = lax.ppermute(up, "stream", ring("stream", 1))
     from_high = lax.ppermute(down, "stream", ring("stream", -1))
 

time: 19.2 us -> 18 us (0.938)
  the two profiles are of different devices: /device:TPU:3 before, /device:TPU:0 now
where the time goes in v1:
time: 18 us; the launch traced here: 17.9 us
  starting transfers between devices  7.63 us (42%)
  Pallas kernels  6.37 us (35%)
  waiting for transfers between devices  3.15 us (18%)
  between operations  0.7 us (4%)
    ppermute x1, starting transfers between devices, local(): from_above = lax.ppermute(down, 'span', ring('span', -1))  3.52 us
    ppermute x1, starting transfers between devices, local(): from_low = lax.ppermute(up, 'stream', ring('stream', 1))  3.02 us
    pallas_call x1, Pallas kernels, local(): pl.pallas_call(outer_kernel, out_shape=(fine_shape, coarse_shape), in_spe...  2.96 us
    pallas_call x1, Pallas kernels, local(): pl.pallas_call(inner_kernel, out_shape=(fine_shape, coarse_shape, struct(...  2.08 us
    ppermute x1, waiting for transfers between devices, local(): from_low = lax.ppermute(up, 'stream', ring('stream', 1))  2.04 us
    pallas_call x1, Pallas kernels, local(): pl.pallas_call(lambda *refs: pack_x_kernel(sx, *refs), out_shape=(x_messa...  1.15 us
    ppermute x1, waiting for transfers between devices, local(): from_high = lax.ppermute(down, 'stream', ring('stream', -1))  1.11 us
    ppermute x1, starting transfers between devices, local(): from_high = lax.ppermute(down, 'stream', ring('stream', -1))  1.03 us
  transfers between devices with their start and end apart: 4, of which 2 were waited for; matrix products, arithmetic and copies ran while one was open for 0% of the time, Pallas kernels for 12%

profile of v1, /device:TPU:0, one launch (start us, length us, event | category | flops | bytes accessed | tf_op | source)
XLA Modules:
  0.0 17.9 jit_solution(3916816471821509207)
XLA Ops:
  0.6 0.0 copy-start
  0.6 0.0 copy-start.1
  0.6 1.1 %pack_x.1 = (f32[104,128]{1,0:T(8,128)S(1)}, f32[104,128]{1,0:T(8,128)S(1)}) custom-call(f32[6,6,27,128]{3,2,1,0:T(8,128)} %bitcast.4, f32[3,3,27,64]{3,2,1,0:T(8,128)} %bitcast.7), custom_call_target="tpu_custom_call" | custom-call | tf_op jit(solution)/shard_map/pack_x/pallas_call | solution.py:492
  1.8 3.0 %collective-permute-start = (f32[104,128]{1,0:T(8,128)S(1)}, f32[104,128]{1,0:T(8,128)S(1)}, u32[]{:S(2)}, u32[]{:S(2)}) collective-permute-start(f32[104,128]{1,0:T(8,128)S(1)} %get-tuple-element.18), channel_id=1, source_target_pairs={{0,8},{8,16},{16,24},{24,0},{1,9},{9,17},{17,25},{25,1},{2,10},{10... | collective-permute-start | bytes 159752 | tf_op jit(solution)/shard_map/ppermute | solution.py:507
  4.8 0.0 copy-start.2
  4.8 1.0 %collective-permute-start.1 = (f32[104,128]{1,0:T(8,128)S(1)}, f32[104,128]{1,0:T(8,128)S(1)}, u32[]{:S(2)}, u32[]{:S(2)}) collective-permute-start(f32[104,128]{1,0:T(8,128)S(1)} %get-tuple-element.19), channel_id=1, source_target_pairs={{0,24},{8,0},{16,8},{24,16},{1,25},{9,1},{17,9},{25,17},{2,26},{10... | collective-permute-start | bytes 159752 | tf_op jit(solution)/shard_map/ppermute | solution.py:508
  5.9 2.0 %collective-permute-done.from_low = f32[104,128]{1,0:T(8,128)S(1)} collective-permute-done((f32[104,128]{1,0:T(8,128)S(1)}, f32[104,128]{1,0:T(8,128)S(1)}, u32[]{:S(2)}, u32[]{:S(2)}) %collective-permute-start) | collective-permute-done | bytes 53280 | tf_op jit(solution)/shard_map/ppermute | solution.py:507
  7.9 1.1 %collective-permute-done.1.from_high = f32[104,128]{1,0:T(8,128)S(1)} collective-permute-done((f32[104,128]{1,0:T(8,128)S(1)}, f32[104,128]{1,0:T(8,128)S(1)}, u32[]{:S(2)}, u32[]{:S(2)}) %collective-permute-start.1) | collective-permute-done | bytes 53280 | tf_op jit(solution)/shard_map/ppermute | solution.py:508
  9.0 0.0 copy-done
  9.0 0.0 copy-done.1
  9.0 0.2 pack_y.1
  9.2 0.0 copy-start.3
  9.2 0.1 collective-permute-start.2
  9.2 0.0 copy-start.4
  9.3 3.5 %collective-permute-start.3 = (f32[144,128]{1,0:T(8,128)S(1)}, f32[144,128]{1,0:T(8,128)S(1)}, u32[]{:S(2)}, u32[]{:S(2)}) collective-permute-start(f32[144,128]{1,0:T(8,128)S(1)} %get-tuple-element.21), channel_id=1, source_target_pairs={{0,7},{1,0},{2,1},{3,2},{4,3},{5,4},{6,5},{7,6},{8,15},{9,8},{10,9... | collective-permute-start | bytes 221192 | tf_op jit(solution)/shard_map/ppermute | solution.py:520
  12.8 0.0 copy-done.2
  12.8 0.0 copy-done.3
  12.8 0.0 copy-done.4
  12.8 2.1 %inner.1 = (f32[6,6,27,128]{3,2,1,0:T(8,128)}, f32[3,3,27,64]{3,2,1,0:T(8,128)}, f32[27,4,8,128]{3,2,1,0:T(8,128)S(1)}, f32[27,3,8,128]{3,2,1,0:T(8,128)S(1)}, f...) custom-call(f32[6,6,27,128]{3,2,1,0:T(8,128)S(1)} %bitcast.6, ...), custom_call_target="tpu_custom_call" | custom-call | flops 20000000 | bytes 1000000 | tf_op jit(solution)/shard_map/inner/pallas_call | solution.py:523
  14.9 0.0 collective-permute-done.2.from_below
  14.9 0.0 collective-permute-done.3.from_above
  14.9 3.0 %outer.1 = (f32[6,6,27,128]{3,2,1,0:T(8,128)}, f32[3,3,27,64]{3,2,1,0:T(8,128)}) custom-call(f32[144,128]{1,0:T(8,128)S(1)} %collective-permute-done.2.from_below, f32[144,128]{1,0:T(8,128)S(1)} %collective-permute-done.3.from_above, f32[27,2,8,128]{3,2,1,0:T(8,128)S(1)} %get-tuple-element.22.w_edge, ...), custom_call_target="tpu_custom_call", output_to_operand_aliasing={{0}: (11, {}), {1}: (12, {})} | custom-call | tf_op jit(solution)/shard_map/outer/pallas_call | solution.py:547
Async XLA Ops:
  0.6 8.4 %copy-start = (f32[27,6,6,128]{3,0,2,1:T(8,128)S(1)}, f32[27,6,6,128]{3,0,2,1:T(8,128)}, u32[]{:S(2)}) copy-start(f32[27,6,6,128]{3,0,2,1:T(8,128)} %param.5) | copy-start | bytes 1492996
  0.6 8.4 %copy-start.1 = (f32[27,3,3,64]{3,0,2,1:T(8,128)S(1)}, f32[27,3,3,64]{3,0,2,1:T(8,128)}, u32[]{:S(2)}) copy-start(f32[27,3,3,64]{3,0,2,1:T(8,128)} %param.6) | copy-start | bytes 186628
  1.8 6.1 %collective-permute-start = (f32[104,128]{1,0:T(8,128)S(1)}, f32[104,128]{1,0:T(8,128)S(1)}, u32[]{:S(2)}, u32[]{:S(2)}) collective-permute-start(f32[104,128]{1,0:T(8,128)S(1)} %get-tuple-element.18), channel_id=1, source_target_pairs={{0,8},{8,16},{16,24},{24,0},{1,9},{9,17},{17,25},{25,1},{2,10},{10... | collective-permute-start | bytes 159752 | tf_op jit(solution)/shard_map/ppermute | solution.py:507
  4.8 8.0 %copy-start.2 = (s32[6,6,128]{2,1,0:T(8,128)S(1)}, s32[6,6,128]{2,1,0:T(8,128)}, u32[]{:S(2)}) copy-start(s32[6,6,128]{2,1,0:T(8,128)} %obstacle.1) | copy-start | bytes 55300
  4.8 4.2 %collective-permute-start.1 = (f32[104,128]{1,0:T(8,128)S(1)}, f32[104,128]{1,0:T(8,128)S(1)}, u32[]{:S(2)}, u32[]{:S(2)}) collective-permute-start(f32[104,128]{1,0:T(8,128)S(1)} %get-tuple-element.19), channel_id=1, source_target_pairs={{0,24},{8,0},{16,8},{24,16},{1,25},{9,1},{17,9},{25,17},{2,26},{10... | collective-permute-start | bytes 159752 | tf_op jit(solution)/shard_map/ppermute | solution.py:508
  9.2 3.6 %copy-start.3 = (s32[4,8]{1,0:T(4,128)S(1)}, s32[4,8]{1,0:T(4,128)}, u32[]{:S(2)}) copy-start(s32[4,8]{1,0:T(4,128)} %level.3) | copy-start | bytes 388
  9.2 5.7 %collective-permute-start.2 = (f32[144,128]{1,0:T(8,128)S(1)}, f32[144,128]{1,0:T(8,128)S(1)}, u32[]{:S(2)}, u32[]{:S(2)}) collective-permute-start(f32[144,128]{1,0:T(8,128)S(1)} %get-tuple-element.20), channel_id=1, source_target_pairs={{0,1},{1,2},{2,3},{3,4},{4,5},{5,6},{6,7},{7,0},{8,9},{9,10},{10,1... | collective-permute-start | bytes 221192 | tf_op jit(solution)/shard_map/ppermute | solution.py:519
  9.2 3.5 %copy-start.4 = (f32[27]{0:T(128)S(1)}, f32[27]{0:T(128)}, u32[]{:S(2)}) copy-start(f32[27]{0:T(128)} %rates.1) | copy-start | bytes 328
  9.3 5.6 %collective-permute-start.3 = (f32[144,128]{1,0:T(8,128)S(1)}, f32[144,128]{1,0:T(8,128)S(1)}, u32[]{:S(2)}, u32[]{:S(2)}) collective-permute-start(f32[144,128]{1,0:T(8,128)S(1)} %get-tuple-element.21), channel_id=1, source_target_pairs={{0,7},{1,0},{2,1},{3,2},{4,3},{5,4},{6,5},{7,6},{8,15},{9,8},{10,9... | collective-permute-start | bytes 221192 | tf_op jit(solution)/shard_map/ppermute | solution.py:520

commit v2 on v1

v2 whole, which is shorter than its diff:
```python
import jax
import jax.numpy as jnp
from jax import lax
from jax.experimental import pallas as pl
from jax.experimental.pallas import tpu as pltpu
from jax.sharding import PartitionSpec as P

F32 = jnp.float32
I32 = jnp.int32
BF16 = jnp.bfloat16
Q = 27
QPAD = 32
LANES = 128
OCTETS = [(8 * o, min(8, Q - 8 * o)) for o in range(4)]
STEP = [(q // 9 - 1, q // 3 % 3 - 1, q % 3 - 1) for q in range(Q)]
HIGH_X = [q for q in range(Q) if STEP[q][0] == 1]
LOW_X = [q for q in range(Q) if STEP[q][0] == -1]
HIGH_Y = [q for q in range(Q) if STEP[q][1] == 1]
LOW_Y = [q for q in range(Q) if STEP[q][1] == -1]
EVEN = [9 * a + 3 * b + c for a in (0, 2) for b in (0, 2) for c in (0, 2)]

VMEM = pl.BlockSpec(memory_space=pltpu.VMEM)
SMEM = pl.BlockSpec(memory_space=pltpu.SMEM)
ANY = pl.BlockSpec(memory_space=pl.ANY)
LIMIT = 16 << 20

LEV_BELOW, LEV_ROW, LEV_ABOVE = 0, 1, 2
LEV_X_LOW, LEV_X_HIGH, LEV_OWN, LEV_Y_LOW, LEV_Y_HIGH = 3, 4, 5, 6, 7

X_FINE, X_MIDDLE = Q, Q + 9
Y_SECOND, Y_THIRD, Y_CORNER = Q, 2 * Q, 2 * Q + 16
Y_ROWS = 80


def fine_slot(k):
    ex = k // 3 - 1
    if ex == 0:
        return 6 * (k % 3), 6, 1
    return 36 + 7 * (k % 3 if ex < 0 else 3 + k % 3), 7, (1 if ex < 0 else 0)


def params(**more):
    return pltpu.CompilerParams(vmem_limit_bytes=LIMIT, **more)


def struct(shape, dtype=F32):
    return jax.ShapeDtypeStruct(shape, dtype)


def ring(axis, by):
    peers = lax.axis_size(axis)
    return [(i, (i + by) % peers) for i in range(peers)]


def roll_lane(v, by):
    return v if by == 0 else pltpu.roll(v, by % v.shape[1], 1)


def roll_sub(v, by):
    return v if by == 0 else pltpu.roll(v, by % v.shape[0], 0)


def iota(axis, shape=(8, LANES)):
    return lax.broadcasted_iota(I32, shape, axis)


def row8(ref, at):
    return jnp.broadcast_to(ref[at : at + 1], (8, LANES))


def dot_exact(x, m):
    high = x.astype(BF16)
    rest = x - high.astype(F32)
    middle = rest.astype(BF16)
    low = (rest - middle.astype(F32)).astype(BF16)
    return sum(jnp.dot(p, m, preferred_element_type=F32) for p in (low, middle, high))


def pair_of(i):
    a = (i + 1) >> 1
    return a, a + (1 if (i + 1) & 1 else -1)


def blend(a, b):
    return 0.75 * a + 0.25 * b


def pack_x_kernel(fine, coarse, level, up, down, f_low, f_high, c_low, c_high, lev, sems):
    sx, sy, cx = fine.shape[0], fine.shape[1], coarse.shape[0]
    copies = [
        pltpu.make_async_copy(level, lev, sems.at[4]),
        pltpu.make_async_copy(fine.at[sx - 1], f_high, sems.at[0]),
        pltpu.make_async_copy(coarse.at[cx - 1], c_high, sems.at[1]),
        pltpu.make_async_copy(fine.at[0], f_low, sems.at[2]),
        pltpu.make_async_copy(coarse.at[0], c_low, sems.at[3]),
    ]
    for c in copies:
        c.start()
    for c in copies:
        c.wait()
    cy, nzc = c_low.shape[0], c_low.shape[2]
    n_row = lev.shape[0]
    row, col = lax.axis_index("stream"), lax.axis_index("span")
    own = lev[row, col]
    for out, f, c, qs, to in ((up, f_high, c_high, HIGH_X, row + 1), (down, f_low, c_low, LOW_X, row + n_row - 1)):
        out[0:Q, 0:nzc] = c[0]
        out[0:Q, nzc : 2 * nzc] = c[cy - 1]
        for y in range(sy):
            out[X_FINE + 9 * y : X_FINE + 9 * y + 9] = f[y, qs[0] : qs[0] + 9]

        @pl.when((own != 1) | (lev[lax.rem(to, n_row), col] != 1))
        def _(out=out, c=c):
            out[X_MIDDLE : X_MIDDLE + 16, 0:nzc] = c[1, 0:16]
            out[X_MIDDLE : X_MIDDLE + Q - 16, nzc : 2 * nzc] = c[1, 16:Q]


def gain_of(q):
    return (1.0 if q // 9 == 0 else 1.0 / 3.0) * (1.0 if q // 3 % 3 == 0 else 1.0 / 3.0) * (
        1.0 if q % 3 == 0 else 1.0 / 3.0)


def tables_kernel(coarse, obstacle, level, rates, levels, coef, flags, c_wall, c_wide, refine, thin):
    cx, cy, nzc = coarse.shape[0], coarse.shape[1], coarse.shape[3]
    sx, sy, nz = obstacle.shape
    row, col = lax.axis_index("stream"), lax.axis_index("span")
    n_row, n_col = level.shape
    at_row = [lax.rem(row + n_row - 1, n_row), row, lax.rem(row + 1, n_row)]
    at_col = [lax.rem(col + n_col - 1, n_col), col, lax.rem(col + 1, n_col)]
    lane, sub = iota(1), iota(0)
    for k in range(3):
        levels[k] = jnp.where(sub == 0, level[at_row[0], at_col[k]],
                              jnp.where(sub == sx + 1, level[at_row[2], at_col[k]], level[at_row[1], at_col[k]]))
    for k, (r, c) in ((LEV_X_LOW, (0, 1)), (LEV_X_HIGH, (2, 1)), (LEV_OWN, (1, 1)), (LEV_Y_LOW, (1, 0)),
                      (LEV_Y_HIGH, (1, 2))):
        levels[k] = jnp.full((8, LANES), level[at_row[r], at_col[c]], I32)
    refined = levels[LEV_OWN] == 1
    for q in range(Q):
        s = jnp.full((8, LANES), rates[q], F32)
        s = jnp.where(refined, s, 1.0 / (2.0 / s - 0.5))
        coef[q] = 0.125 - 0.125 * s
        if q in EVEN:
            coef[Q + EVEN.index(q)] = (0.125 * gain_of(q)) * s
    planes = []
    for k, y in enumerate((sy // 2 - 1, sy // 2)):
        v = jnp.zeros((8, LANES), I32)
        for x in (sx // 2 - 1, sx // 2):
            v = jnp.where(sub == x + 1, jnp.broadcast_to(obstacle[x, y : y + 1, :], (8, LANES)), v)
        flags[k] = v
        planes.append(v)
    both = jnp.maximum(planes[0], planes[1])
    both = jnp.maximum(both, roll_sub(both, -1))
    both = jnp.maximum(both, roll_lane(both, -1))
    both = jnp.take_along_axis(both, (2 * lane) & (LANES - 1), axis=1)
    both = jnp.broadcast_to(both[sx // 2 : sx // 2 + 1], (8, LANES))
    c_wall[...] = jnp.where((sub == 1 + cx // 2) & (lane < nzc), both, 0)
    shape = (2 * nzc, 2 * nz)
    i, l = iota(0, shape), iota(1, shape)
    half, l = l // nz, l % nz
    za = (l >> 1) + half * nzc
    zb = jnp.clip((l >> 1) + jnp.where((l & 1) == 1, 1, -1), 0, nzc - 1) + half * nzc
    refine[...] = (jnp.where(i == za, 0.75, 0.0) + jnp.where(i == zb, 0.25, 0.0)).astype(BF16)
    shape = (nz, nz)
    thin[...] = jnp.where((iota(0, shape) >> 1) == iota(1, shape), 0.125, 0.0).astype(BF16)
    for Y in range(cy):
        for X in range(cx):
            c_wide[Y, X, 0:Q] = dot_exact(coarse[X, Y], refine[0:nzc, 0:nz])


def fine_plane(fine, from_low, from_high, y, mixed=None):
    sx = fine.shape[0]
    base = X_FINE + 9 * y
    rows = [None] * Q
    for q0, n in OCTETS:
        cells = [fine[x, y, q0 : q0 + n] for x in range(sx)]
        low = high = cells[0]
        if q0 == 16:
            low = from_low[base - 2 : base + 6]
        if q0 == 24:
            low = from_low[base + 6 : base + 9]
        if q0 == 0:
            high = from_high[base : base + 8]
        if q0 == 8:
            high = row8(from_high, base + 8)
        if mixed is not None:
            if q0 >= 16:
                low = mixed(0, q0, n, low)
            else:
                high = mixed(1, q0, n, high)
        tile = jnp.swapaxes(jnp.stack([low, *cells, high]), 0, 1)
        for k in range(n):
            rows[q0 + k] = tile[k]
    return rows


def coarse_plane(tile_of):
    rows = [None] * Q
    for q0, n in OCTETS:
        tiles = [tile_of(I, q0, n) for I in range(5)]
        tile = jnp.swapaxes(jnp.stack(tiles + tiles[:3]), 0, 1)
        for k in range(n):
            rows[q0 + k] = tile[k]
    return rows


def pack_y_kernel(fine, coarse, from_low, from_high, levels, up, down, w_edge):
    sy, cy, nzc = fine.shape[1], coarse.shape[1], coarse.shape[3]
    low_half = iota(1, (Q, LANES)) < nzc
    own = levels[LEV_OWN] == 1
    for out, e, y, Y, qs, to in ((up, 1, sy - 1, cy - 1, HIGH_Y, LEV_Y_HIGH), (down, 0, 0, 0, LOW_Y, LEV_Y_LOW)):
        both = own & (levels[to] == 1)
        g_low, g_high = from_low[0:Q], from_high[0:Q]
        if e == 0:
            g_high = roll_lane(g_high, nzc)
        else:
            g_low = roll_lane(g_low, nzc)
        out[0:Q] = g_low
        out[0:Q, nzc : 2 * nzc] = coarse[0, Y]
        out[Y_SECOND : Y_SECOND + Q] = g_high
        out[Y_SECOND : Y_SECOND + Q, 0:nzc] = coarse[2, Y]
        out[Y_THIRD : Y_THIRD + 16, 0:nzc] = coarse[1, Y, 0:16]
        out[Y_THIRD : Y_THIRD + Q - 16, nzc : 2 * nzc] = coarse[1, Y, 16:Q]
        rows = fine_plane(fine, from_low, from_high, y)
        for q in range(Q):
            w_edge[q, e] = rows[q]
        for k in range(3):
            out[Y_CORNER + k : Y_CORNER + k + 1] = rows[qs[6 + k]][0:1]
            out[Y_CORNER + 3 + k : Y_CORNER + 4 + k] = rows[qs[k]][7:8]
        for k, q in enumerate(qs):
            at, n, s = fine_slot(k)
            out[at : at + n] = jnp.where(both[0:n], rows[q][s : s + n], out[at : at + n])


def forward(m0, m1, m2):
    pair = m0 + m2
    return pair + 4.0 * m1, m2 - m0, pair


ALONG_Y = [(9 * a + c, 3) for a in range(3) for c in range(3)]
ALONG_Z = [(9 * a + 3 * b, 1) for a in range(3) for b in range(3)]
ALONG_X = [(r, 9) for r in range(9)]


def collide(g, coef):
    t = [None] * Q
    for r in range(9):
        t[r], t[9 + r], t[18 + r] = forward(g[r], g[9 + r], g[18 + r])
    cols = [(t[c] + t[6 + c]) + 4.0 * t[3 + c] for c in range(3)]
    density = (cols[0] + cols[2]) + 4.0 * cols[1]
    inv = 1.0 / density
    rows = [(t[3 * b] + t[3 * b + 2]) + 4.0 * t[3 * b + 1] for b in (0, 2)]
    uy = (rows[1] - rows[0]) * inv
    uz = (cols[2] - cols[0]) * inv
    dcols = [(t[9 + c] + t[15 + c]) + 4.0 * t[12 + c] for c in range(3)]
    ux = ((dcols[0] + dcols[2]) + 4.0 * dcols[1]) * inv
    for r in range(9):
        t0, d, pair = t[r], t[9 + r], t[18 + r]
        t1 = d - ux * t0
        t[9 + r], t[18 + r] = t1, pair - ux * (d + t1)
    for u, lines in ((uy, ALONG_Y), (uz, ALONG_Z)):
        for at, by in lines:
            t0, d, pair = forward(t[at], t[at + by], t[at + 2 * by])
            t1 = d - u * t0
            t[at], t[at + by], t[at + 2 * by] = t0, t1, pair - u * (d + t1)
    for q in range(Q):
        t[q] = coef[q] * t[q]
        if q in EVEN:
            t[q] = t[q] + coef[Q + EVEN.index(q)] * density
    for u, lines in ((uz, ALONG_Z), (uy, ALONG_Y), (ux, ALONG_X)):
        for at, by in lines:
            t0, t1, t2 = t[at], t[at + by], t[at + 2 * by]
            d = t1 + u * t0
            s = t2 + u * (t1 + d)
            t[at], t[at + by], t[at + 2 * by] = s - d, 0.5 * (t0 - s), s + d
    return t


def pull(source, center, step_mask):
    out = []
    for q in range(Q):
        ex, ey, ez = STEP[q]
        v = roll_lane(roll_sub(source(q), ex), ez)
        mask = step_mask(ex, ey, ez)
        if mask is not None:
            v = jnp.where(mask, center(26 - q), v)
        out.append(v)
    return out


def bounce_mask(height, wall_of):
    lane = iota(1)
    edges = {1: lane == 0, -1: lane == height - 1}

    def mask_of(ex, ey, ez):
        m = None
        if (ex, ey, ez) == (0, 0, 0):
            return None
        wall = wall_of(ey)
        if wall is not None:
            m = roll_lane(roll_sub(wall, ex), ez) == 1
        if ez != 0:
            m = edges[ez] if m is None else m | edges[ez]
        return m

    return mask_of


def wall_plane(flags, y, first):
    def wall_of(ey):
        k = y - ey - first
        return flags[k] if k in (0, 1) else None

    return wall_of


def store_rows(rows, out, t, xs, width):
    for q0, n in OCTETS:
        tile = jnp.swapaxes(jnp.stack(rows[q0 : q0 + n]), 0, 1)
        for k, x in enumerate(xs):
            out[k, t, q0 : q0 + n] = tile[x][:, 0:width]


def coalesce(buf, t, out, at, thin):
    nzc = out.shape[3]
    for X in range(out.shape[0]):
        s = (buf[2 * X, t] + buf[2 * X + 1, t]) + (buf[2 * X, t + 1] + buf[2 * X + 1, t + 1])
        out[X, at] = dot_exact(s, thin[...])[:, 0:nzc]


def coarse_step(plane, J, wall, coef, buf, at, nzc, cx, wall_row):
    mask_of = bounce_mask(nzc, lambda ey: wall if J - ey == wall_row else None)
    new = collide(pull(lambda q: plane(q, J - STEP[q][1]), lambda q: plane(q, J), mask_of), coef)
    if J == wall_row:
        stay = wall == 1
        new = [jnp.where(stay, plane(q, J), new[q]) for q in range(Q)]
    store_rows(new, buf, at, range(1, cx + 1), nzc)


def inner_kernel(fine, coarse, from_low, from_high, levels, coef, flags, c_wall, c_wide, refine, thin,
                 out, c_out, w_in, ex_side, c_all, ghost, ex_mid, f_buf, c_buf, sems):
    sx, sy, nz = fine.shape[0], fine.shape[1], fine.shape[3]
    cx, cy, nzc = coarse.shape[0], coarse.shape[1], coarse.shape[3]
    mid = sy // 2
    own = jnp.max(levels[LEV_OWN])
    for side, msg in enumerate((from_low, from_high)):
        v = dot_exact(msg[0:Q], refine[...])
        ghost[side, 0, 0:Q] = v[:, 0:nz]
        ghost[side, cy - 1, 0:Q] = v[:, nz : 2 * nz]
        v = dot_exact(msg[X_MIDDLE : X_MIDDLE + 16], refine[...])
        ghost[side, 1, 0:16] = v[:, 0:nz]
        ghost[side, 1, 16:Q] = v[0 : Q - 16, nz : 2 * nz]

    def wide(J, I):
        if I == 0:
            return ghost[0, J - 1]
        if I == cx + 1:
            return ghost[1, J - 1]
        return c_wide[J - 1, I - 1]

    for J in range(1, cy + 1):
        for i in range(sx + 2):
            a, b = pair_of(i)
            v = blend(wide(J, a), wide(J, b))
            if J == 2:
                ex_mid[i] = v
            else:
                ex_side[J // 2, i] = v

    def exploded(J, i):
        return ex_mid.at[i] if J == 2 else ex_side.at[J // 2, i]

    copies = [pltpu.make_async_copy(f_buf.at[:, pl.ds(1, 2)], out.at[:, pl.ds(mid - 1, 2)], sems.at[0]),
              pltpu.make_async_copy(c_buf, c_out.at[:, pl.ds(cy // 2, 1)], sems.at[1]),
              pltpu.make_async_copy(f_buf, out.at[:, pl.ds(1, 4)], sems.at[0])]

    @pl.when(own == 1)
    def _():
        refined = (levels[LEV_X_LOW] == 1, levels[LEV_X_HIGH] == 1)
        for y in range(1, sy - 1):
            a, b = pair_of(y + 1)

            def mixed(side, q0, n, tile):
                i = 0 if side == 0 else sx + 1
                e = blend(exploded(a, i)[q0 : q0 + n], exploded(b, i)[q0 : q0 + n])
                return jnp.where(refined[side][0:n], tile, e)

            rows = fine_plane(fine, from_low, from_high, y, mixed)
            for q in range(Q):
                w_in[q, y - 1] = rows[q]
        for y in (mid - 1, mid):
            pulled = pull(lambda q: w_in[q, y - 1 - STEP[q][1]], lambda q: w_in[q, y - 1],
                          bounce_mask(nz, wall_plane(flags, y, mid - 1)))
            new = collide(pulled, coef)
            stay = flags[y - mid + 1] == 1
            new = [jnp.where(stay, w_in[q, y - 1], new[q]) for q in range(Q)]
            store_rows(new, f_buf, y - 1, range(1, sx + 1), nz)
        copies[0].start()
        coalesce(f_buf, 1, c_buf, 0, thin)
        copies[1].start()
        copies[0].wait()

    @pl.when(own != 1)
    def _():
        for y in range(1, sy - 1):
            a, b = pair_of(y + 1)
            for x in range(sx):
                f_buf[x, y - 1] = blend(exploded(a, x + 1)[0:Q], exploded(b, x + 1)[0:Q])
        copies[2].start()

        def tile_of(Y):
            def tile(I, q0, n):
                if 1 <= I <= cx:
                    return coarse[I - 1, Y, q0 : q0 + n]
                msg = from_low if I == 0 else from_high
                if Y != 1:
                    v = msg[q0 : q0 + n]
                    return (v if Y == 0 else roll_lane(v, nzc))[:, 0:nzc]
                if q0 < 16:
                    return msg[X_MIDDLE + q0 : X_MIDDLE + q0 + n, 0:nzc]
                return roll_lane(msg[X_MIDDLE + q0 - 16 : X_MIDDLE + q0 - 16 + n], nzc)[:, 0:nzc]

            return tile

        for Y in range(cy):
            for q, v in enumerate(coarse_plane(tile_of(Y))):
                c_all[q, Y, :, 0:nzc] = v
        coarse_step(lambda q, J: c_all[q, J - 1], 2, c_wall[...], coef, c_buf, 0, nzc, cx, 2)
        copies[1].start()
        copies[2].wait()

    copies[1].wait()


def outer_kernel(from_below, from_above, w_edge, w_in, c_all, ex_side, levels, coef, flags, c_wall, refine, thin,
                 _out_in, _c_in, out, c_out, wide, ex_g, w_g, w_e, c_g, f_buf, c_buf, sems):
    sx, sy, nz = out.shape[0], out.shape[1], out.shape[3]
    cx, cy, nzc = c_out.shape[0], c_out.shape[1], c_out.shape[3]
    own = jnp.max(levels[LEV_OWN])
    sub = iota(0)
    for e, msg in enumerate((from_below, from_above)):
        v = dot_exact(msg[0:72], refine[...])
        wide[0, 0:Q] = v[0:Q, 0:nz]
        wide[1, 0:Q] = v[0:Q, nz : 2 * nz]
        wide[3, 0:Q] = v[Y_SECOND : Y_SECOND + Q, 0:nz]
        wide[4, 0:Q] = v[Y_SECOND : Y_SECOND + Q, nz : 2 * nz]
        wide[2, 0:16] = v[Y_THIRD : Y_THIRD + 16, 0:nz]
        wide[2, 16:Q] = v[Y_THIRD : Y_THIRD + Q - 16, nz : 2 * nz]
        for i in range(sx + 2):
            a, b = pair_of(i)
            ex_g[e, i] = blend(wide[a], wide[b])

    def plane_copy(y):
        return pltpu.make_async_copy(f_buf.at[:, pl.ds(y, 1)], out.at[:, pl.ds(y, 1)], sems.at[y])

    def coarse_copy(e):
        return pltpu.make_async_copy(c_buf.at[:, pl.ds(e, 1)], c_out.at[:, pl.ds((cy - 1) * e, 1)],
                                     sems.at[sy + e])

    @pl.when(own == 1)
    def _():
        for e, msg in enumerate((from_below, from_above)):
            qs = HIGH_Y if e == 0 else LOW_Y
            ghost_j, edge_j = (0, 1) if e == 0 else (sy + 1, sy)
            far = levels[LEV_BELOW if e == 0 else LEV_ABOVE] == 1
            near = levels[LEV_Y_LOW if e == 0 else LEV_Y_HIGH] == 1
            for q0, n in OCTETS:
                tiles = [blend(ex_g[e, i, q0 : q0 + n], ex_side[e, i, q0 : q0 + n]) for i in range(sx + 2)]
                tile = jnp.swapaxes(jnp.stack(tiles), 0, 1)
                for k, q in enumerate(qs):
                    if q0 <= q < q0 + n:
                        at, _, s = fine_slot(k)
                        v = roll_sub(msg[at : at + 8], s)
                        if STEP[q][0] != 0:
                            corner = Y_CORNER + k % 3 + (0 if STEP[q][0] > 0 else 3)
                            v = jnp.where(near, v, row8(msg, corner))
                        w_g[k] = jnp.where(far, v, tile[q - q0])
            coarse_low = (levels[LEV_X_LOW] != 1) & (sub == 0)
            coarse_high = (levels[LEV_X_HIGH] != 1) & (sub == sx + 1)
            v_low = blend(ex_side[e, 0], ex_g[e, 0])
            v_high = blend(ex_side[e, sx + 1], ex_g[e, sx + 1])
            for q in range(Q):
                v = w_edge[q, e]
                if STEP[q][0] > 0:
                    v = jnp.where(coarse_low, jnp.broadcast_to(v_low[q : q + 1], (8, LANES)), v)
                if STEP[q][0] < 0:
                    v = jnp.where(coarse_high, jnp.broadcast_to(v_high[q : q + 1], (8, LANES)), v)
                w_e[q] = v

            def plane(q, j):
                if j == ghost_j:
                    return w_g[qs.index(q)]
                if j == edge_j:
                    return w_e[q]
                return w_in[q, j - 2]

            for y in ((0, 1) if e == 0 else (sy - 1, sy - 2)):
                pulled = pull(lambda q: plane(q, y + 1 - STEP[q][1]), lambda q: plane(q, y + 1),
                              bounce_mask(nz, wall_plane(flags, y, sy // 2 - 1)))
                store_rows(collide(pulled, coef), f_buf, y, range(1, sx + 1), nz)
                plane_copy(y).start()
            coalesce(f_buf, 0 if e == 0 else sy - 2, c_buf, e, thin)
            coarse_copy(e).start()
        plane_copy(1).wait()
        plane_copy(sy - 2).wait()

    @pl.when(own != 1)
    def _():
        wall = c_wall[...]

        for e, msg in enumerate((from_below, from_above)):
            y = 0 if e == 0 else sy - 1
            for x in range(sx):
                f_buf[x, y] = blend(ex_side[e, x + 1, 0:Q], ex_g[e, x + 1, 0:Q])
            plane_copy(y).start()

            def tile(I, q0, n):
                at = Y_SECOND if I >= 3 else 0
                if I == 2:
                    at = Y_THIRD - (16 if q0 >= 16 else 0)
                v = msg[at + q0 : at + q0 + n]
                if I in (1, 4) or (I == 2 and q0 >= 16):
                    v = roll_lane(v, nzc)
                return v[:, 0:nzc]

            for q, v in enumerate(coarse_plane(tile)):
                c_g[q, e, :, 0:nzc] = v

        def plane(q, J):
            if J == 0:
                return c_g[q, 0]
            if J == cy + 1:
                return c_g[q, 1]
            return c_all[q, J - 1]

        for e in range(2):
            coarse_step(plane, 1 if e == 0 else cy, wall, coef, c_buf, e, nzc, cx, 2)
            coarse_copy(e).start()

    plane_copy(0).wait()
    plane_copy(sy - 1).wait()
    for e in range(2):
        coarse_copy(e).wait()


def cost(flops, nbytes):
    return pl.CostEstimate(flops=flops, bytes_accessed=nbytes, transcendentals=0)


def in_hbm(x):
    return pltpu.with_memory_space_constraint(x, pltpu.HBM)


def local(fine_pops, coarse_pops, obstacle, block_level, relax_rates):
    fine = jnp.transpose(fine_pops, (1, 2, 0, 3))
    coarse = jnp.transpose(coarse_pops, (1, 2, 0, 3))
    sx, sy, _, nz = fine.shape
    cx, cy, _, nzc = coarse.shape

    x_message = struct((8 * ((X_FINE + 9 * sy + 7) // 8), LANES))
    up, down = pl.pallas_call(
        pack_x_kernel,
        out_shape=(x_message, x_message),
        in_specs=[ANY] * 3,
        out_specs=(VMEM, VMEM),
        scratch_shapes=[
            pltpu.VMEM((sy, Q, nz), F32),
            pltpu.VMEM((sy, Q, nz), F32),
            pltpu.VMEM((cy, Q, nzc), F32),
            pltpu.VMEM((cy, Q, nzc), F32),
            pltpu.SMEM(block_level.shape, I32),
            pltpu.SemaphoreType.DMA((5,)),
        ],
        compiler_params=params(),
        name="pack_x",
    )(in_hbm(fine), in_hbm(coarse), in_hbm(block_level))
    from_low = lax.ppermute(up, "stream", ring("stream", 1))
    from_high = lax.ppermute(down, "stream", ring("stream", -1))

    levels, coef, flags, c_wall, c_wide, refine, thin = pl.pallas_call(
        tables_kernel,
        out_shape=(
            struct((8, 8, LANES), I32),
            struct((Q + len(EVEN), 8, LANES)),
            struct((2, 8, LANES), I32),
            struct((8, LANES), I32),
            struct((cy, cx, QPAD, nz)),
            struct((2 * nzc, 2 * nz), BF16),
            struct((nz, nz), BF16),
        ),
        in_specs=[VMEM] * 2 + [SMEM] * 2,
        out_specs=(VMEM,) * 7,
        compiler_params=params(),
        cost_estimate=cost(10_000_000, 1_000_000),
        name="tables",
    )(coarse, obstacle, block_level, relax_rates)

    y_message = struct((Y_ROWS, LANES))
    up, down, w_edge = pl.pallas_call(
        pack_y_kernel,
        out_shape=(y_message, y_message, struct((Q, 2, 8, LANES))),
        in_specs=[VMEM] * 5,
        out_specs=(VMEM,) * 3,
        compiler_params=params(),
        name="pack_y",
    )(fine, coarse, from_low, from_high, levels)
    from_below = lax.ppermute(up, "span", ring("span", 1))
    from_above = lax.ppermute(down, "span", ring("span", -1))

    fine_shape, coarse_shape = struct(fine.shape), struct(coarse.shape)
    out, c_out, w_in, ex_side, c_all = pl.pallas_call(
        inner_kernel,
        out_shape=(
            fine_shape,
            coarse_shape,
            struct((Q, sy - 2, 8, LANES)),
            struct((2, sx + 2, QPAD, nz)),
            struct((Q, cy, 8, LANES)),
        ),
        in_specs=[VMEM] * 11,
        out_specs=(ANY, ANY) + (VMEM,) * 3,
        scratch_shapes=[
            pltpu.VMEM((2, cy, QPAD, nz), F32),
            pltpu.VMEM((sx + 2, QPAD, nz), F32),
            pltpu.VMEM((sx, sy - 2, Q, nz), F32),
            pltpu.VMEM((cx, 1, Q, nzc), F32),
            pltpu.SemaphoreType.DMA((2,)),
        ],
        compiler_params=params(),
        cost_estimate=cost(20_000_000, 1_000_000),
        name="inner",
    )(fine, coarse, from_low, from_high, levels, coef, flags, c_wall, c_wide, refine, thin)

    out, c_out = pl.pallas_call(
        outer_kernel,
        out_shape=(fine_shape, coarse_shape),
        in_specs=[VMEM] * 12 + [ANY, ANY],
        out_specs=(ANY, ANY),
        scratch_shapes=[
            pltpu.VMEM((5, QPAD, nz), F32),
            pltpu.VMEM((2, sx + 2, QPAD, nz), F32),
            pltpu.VMEM((9, 8, LANES), F32),
            pltpu.VMEM((Q, 8, LANES), F32),
            pltpu.VMEM((Q, 2, 8, LANES), F32),
            pltpu.VMEM((sx, sy, Q, nz), F32),
            pltpu.VMEM((cx, 2, Q, nzc), F32),
            pltpu.SemaphoreType.DMA((sy + 2,)),
        ],
        input_output_aliases={12: 0, 13: 1},
        compiler_params=params(),
        name="outer",
    )(from_below, from_above, w_edge, w_in, c_all, ex_side, levels, coef, flags, c_wall, refine, thin,
      out, c_out)
    return jnp.transpose(out, (2, 0, 1, 3)), jnp.transpose(c_out, (2, 0, 1, 3))


def solution(mesh):
    placed = (
        P(None, "stream", "span", None),
        P(None, "stream", "span", None),
        P("stream", "span", None),
        P(),
        P(),
    )
    return jax.shard_map(
        local,
        mesh=mesh,
        in_specs=placed,
        out_specs=(P(None, "stream", "span", None), P(None, "stream", "span", None)),
        check_vma=False,
    )
```

time: 18 us -> 16.2 us (0.90)
  waiting for transfers between devices: 3.15 us -> 1.68 us
  Pallas kernels: 6.37 us -> 5.4 us
  local copies, waits for them, and re-layouts: 0.02 us -> 0.75 us
    ppermute x1, waiting for transfers between devices: 2.04 us -> 0.33 us  [local(): from_low = lax.ppermute(up, 'stream', ring('stream', 1))]
    pallas_call x1, Pallas kernels: 2.96 us -> 1.75 us  [local(): pl.pallas_call(outer_kernel, out_shape=(fine_shape, coarse_shape), in_spe...]
    pallas_call x1 -> x2, Pallas kernels: 1.15 us -> 2.11 us  [the longest x1 1.23 us: local(): pl.pallas_call(pack_x_kernel, out_shape=(x_message, x_message), in_specs=...]
    unnamed x10, local copies, waits for them, and re-layouts: 0.02 us -> 0.75 us
    pallas_call x1, Pallas kernels: 2.08 us -> 1.43 us  [local(): pl.pallas_call(inner_kernel, out_shape=(fine_shape, coarse_shape, struct(...]
    ppermute x1, waiting for transfers between devices: 0.01 us -> 0.28 us  [local(): from_below = lax.ppermute(up, 'span', ring('span', 1))]
  transfers between devices with their start and end apart: 4 -> 4, of which waited for: 2 -> 3; matrix products, arithmetic and copies ran while one was open for 0% -> 0% of each run, Pallas kernels for 12% -> 14%
where the time goes in v2:
time: 16.2 us
  starting transfers between devices  7.63 us (47%)
  Pallas kernels  5.4 us (33%)
  waiting for transfers between devices  1.68 us (10%)
  local copies, waits for them, and re-layouts  0.75 us (5%)
  between operations  0.7 us (4%)
    ppermute x1, starting transfers between devices, local(): from_above = lax.ppermute(down, 'span', ring('span', -1))  3.53 us
    ppermute x1, starting transfers between devices, local(): from_low = lax.ppermute(up, 'stream', ring('stream', 1))  3.02 us
    pallas_call x1, Pallas kernels, local(): pl.pallas_call(outer_kernel, out_shape=(fine_shape, coarse_shape), in_spe...  1.75 us
    pallas_call x1, Pallas kernels, local(): pl.pallas_call(inner_kernel, out_shape=(fine_shape, coarse_shape, struct(...  1.43 us
    pallas_call x1, Pallas kernels, local(): pl.pallas_call(pack_x_kernel, out_shape=(x_message, x_message), in_specs=...  1.23 us
    ppermute x1, waiting for transfers between devices, local(): from_high = lax.ppermute(down, 'stream', ring('stream', -1))  1.07 us
    ppermute x1, starting transfers between devices, local(): from_high = lax.ppermute(down, 'stream', ring('stream', -1))  1.02 us
    pallas_call x1, Pallas kernels, local(): pl.pallas_call(tables_kernel, out_shape=(struct((8, 8, LANES), I32), stru...  0.88 us
  transfers between devices with their start and end apart: 4, of which 3 were waited for; matrix products, arithmetic and copies ran while one was open for 0% of the time, Pallas kernels for 14%

profile of v2, /device:TPU:0, one launch (start us, length us, event | category | flops | bytes accessed | tf_op | source)
XLA Modules:
  0.0 16.2 jit_solution(7032077797571378915)
XLA Ops:
  0.6 0.0 copy-start
  0.6 0.0 copy-start.1
  0.6 1.2 %pack_x.1 = (f32[88,128]{1,0:T(8,128)S(1)}, f32[88,128]{1,0:T(8,128)S(1)}) custom-call(f32[6,6,27,128]{3,2,1,0:T(8,128)} %bitcast.4, f32[3,3,27,64]{3,2,1,0:T(8,128)} %bitcast.7, s32[4,8]{1,0:T(4,128)} %level.3), custom_call_target="tpu_custom_call" | custom-call | tf_op jit(solution)/shard_map/pack_x/pallas_call | solution.py:559
  1.9 0.0 copy-start.3
  1.9 0.0 copy-start.4
  1.9 3.0 %collective-permute-start = (f32[88,128]{1,0:T(8,128)S(1)}, f32[88,128]{1,0:T(8,128)S(1)}, u32[]{:S(2)}, u32[]{:S(2)}) collective-permute-start(f32[88,128]{1,0:T(8,128)S(1)} %get-tuple-element.21), channel_id=1, source_target_pairs={{0,8},{8,16},{16,24},{24,0},{1,9},{9,17},{17,25},{25,1},{2,10},{10... | collective-permute-start | bytes 135176 | tf_op jit(solution)/shard_map/ppermute | solution.py:575
  4.9 1.0 %collective-permute-start.1 = (f32[88,128]{1,0:T(8,128)S(1)}, f32[88,128]{1,0:T(8,128)S(1)}, u32[]{:S(2)}, u32[]{:S(2)}) collective-permute-start(f32[88,128]{1,0:T(8,128)S(1)} %get-tuple-element.22), channel_id=1, source_target_pairs={{0,24},{8,0},{16,8},{24,16},{1,25},{9,1},{17,9},{25,17},{2,26},{10... | collective-permute-start | bytes 135176 | tf_op jit(solution)/shard_map/ppermute | solution.py:576
  6.0 0.0 copy-done.1
  6.0 0.0 copy-done.3
  6.0 0.0 copy-done.4
  6.0 0.0 copy-start.2
  6.0 0.7 %copy-done.2 = s32[6,6,128]{2,1,0:T(8,128)S(1)} copy-done((s32[6,6,128]{2,1,0:T(8,128)S(1)}, s32[6,6,128]{2,1,0:T(8,128)}, u32[]{:S(2)}) %copy-start.2) | copy-done | bytes 18456
  6.7 0.9 %tables.1 = (s32[8,8,128]{2,1,0:T(8,128)S(1)}, f32[35,8,128]{2,1,0:T(8,128)S(1)}, s32[2,8,128]{2,1,0:T(8,128)S(1)}, s32[8,128]{1,0:T(8,128)S(1)}, f32[3,3,32,128...) custom-call(f32[3,3,27,64]{3,2,1,0:T(8,128)S(1)} %bitcast.8, ...), custom_call_target="tpu_custom_call" | custom-call | flops 10000000 | bytes 1000000 | tf_op jit(solution)/shard_map/tables/pallas_call | solution.py:578
  7.6 0.3 %collective-permute-done.from_low = f32[88,128]{1,0:T(8,128)S(1)} collective-permute-done((f32[88,128]{1,0:T(8,128)S(1)}, f32[88,128]{1,0:T(8,128)S(1)}, u32[]{:S(2)}, u32[]{:S(2)}) %collective-permute-start) | collective-permute-done | bytes 45088 | tf_op jit(solution)/shard_map/ppermute | solution.py:575
  7.9 1.1 %collective-permute-done.1.from_high = f32[88,128]{1,0:T(8,128)S(1)} collective-permute-done((f32[88,128]{1,0:T(8,128)S(1)}, f32[88,128]{1,0:T(8,128)S(1)}, u32[]{:S(2)}, u32[]{:S(2)}) %collective-permute-start.1) | collective-permute-done | bytes 45088 | tf_op jit(solution)/shard_map/ppermute | solution.py:576
  9.0 0.0 copy-done
  9.0 0.1 pack_y.1
  9.1 0.1 collective-permute-start.2
  9.2 3.5 %collective-permute-start.3 = (f32[80,128]{1,0:T(8,128)S(1)}, f32[80,128]{1,0:T(8,128)S(1)}, u32[]{:S(2)}, u32[]{:S(2)}) collective-permute-start(f32[80,128]{1,0:T(8,128)S(1)} %get-tuple-element.25), channel_id=1, source_target_pairs={{0,7},{1,0},{2,1},{3,2},{4,3},{5,4},{6,5},{7,6},{8,15},{9,8},{10,9... | collective-permute-start | bytes 122888 | tf_op jit(solution)/shard_map/ppermute | solution.py:606
  12.7 1.4 %inner.1 = (f32[6,6,27,128]{3,2,1,0:T(8,128)}, f32[3,3,27,64]{3,2,1,0:T(8,128)}, f32[27,4,8,128]{3,2,1,0:T(8,128)S(1)}, f32[2,8,32,128]{3,2,1,0:T(8,128)S(1)}, f32[27,3,8,128]{3,2,1,0:T(8,128)S(1)}) custom-call(f32[6,6,27,128]{3,2,1,0:T(8,128)S(1)} %bitcast.6, f32[3,3,27,64]{3,2,1,0:T(8,128)S(1)} %bitcast.10, f32[88,128]{1,0:T(8,128)S(1)} %collective-permute-done.from_low, ...), custom_call_target="tpu_custom_call" | custom-call | flops 20000000 | bytes 1000000 | tf_op jit(solution)/shard_map/inner/pallas_call | solution.py:609
  14.1 0.3 %collective-permute-done.2.from_below = f32[80,128]{1,0:T(8,128)S(1)} collective-permute-done((f32[80,128]{1,0:T(8,128)S(1)}, f32[80,128]{1,0:T(8,128)S(1)}, u32[]{:S(2)}, u32[]{:S(2)}) %collective-permute-start.2) | collective-permute-done | bytes 40992 | tf_op jit(solution)/shard_map/ppermute | solution.py:605
  14.4 0.0 collective-permute-done.3.from_above
  14.4 1.8 %outer.1 = (f32[6,6,27,128]{3,2,1,0:T(8,128)}, f32[3,3,27,64]{3,2,1,0:T(8,128)}) custom-call(f32[80,128]{1,0:T(8,128)S(1)} %collective-permute-done.2.from_below, f32[80,128]{1,0:T(8,128)S(1)} %collective-permute-done.3.from_above, f32[27,2,8,128]{3,2,1,0:T(8,128)S(1)} %get-tuple-element.26.w_edge, ...), custom_call_target="tpu_custom_call", output_to_operand_aliasing={{0}: (12, {}), {1}: (13, {})} | custom-call | tf_op jit(solution)/shard_map/outer/pallas_call | solution.py:632
Async XLA Ops:
  0.6 8.4 %copy-start = (f32[27,6,6,128]{3,0,2,1:T(8,128)S(1)}, f32[27,6,6,128]{3,0,2,1:T(8,128)}, u32[]{:S(2)}) copy-start(f32[27,6,6,128]{3,0,2,1:T(8,128)} %param.5) | copy-start | bytes 1492996
  0.6 5.3 %copy-start.1 = (f32[27,3,3,64]{3,0,2,1:T(8,128)S(1)}, f32[27,3,3,64]{3,0,2,1:T(8,128)}, u32[]{:S(2)}) copy-start(f32[27,3,3,64]{3,0,2,1:T(8,128)} %param.6) | copy-start | bytes 186628
  1.9 4.1 %copy-start.3 = (s32[4,8]{1,0:T(4,128)S(1)}, s32[4,8]{1,0:T(4,128)}, u32[]{:S(2)}) copy-start(s32[4,8]{1,0:T(4,128)} %level.3) | copy-start | bytes 388
  1.9 4.1 %copy-start.4 = (f32[27]{0:T(128)S(1)}, f32[27]{0:T(128)}, u32[]{:S(2)}) copy-start(f32[27]{0:T(128)} %rates.1) | copy-start | bytes 328
  1.9 6.0 %collective-permute-start = (f32[88,128]{1,0:T(8,128)S(1)}, f32[88,128]{1,0:T(8,128)S(1)}, u32[]{:S(2)}, u32[]{:S(2)}) collective-permute-start(f32[88,128]{1,0:T(8,128)S(1)} %get-tuple-element.21), channel_id=1, source_target_pairs={{0,8},{8,16},{16,24},{24,0},{1,9},{9,17},{17,25},{25,1},{2,10},{10... | collective-permute-start | bytes 135176 | tf_op jit(solution)/shard_map/ppermute | solution.py:575
  4.9 4.0 %collective-permute-start.1 = (f32[88,128]{1,0:T(8,128)S(1)}, f32[88,128]{1,0:T(8,128)S(1)}, u32[]{:S(2)}, u32[]{:S(2)}) collective-permute-start(f32[88,128]{1,0:T(8,128)S(1)} %get-tuple-element.22), channel_id=1, source_target_pairs={{0,24},{8,0},{16,8},{24,16},{1,25},{9,1},{17,9},{25,17},{2,26},{10... | collective-permute-start | bytes 135176 | tf_op jit(solution)/shard_map/ppermute | solution.py:576
  6.0 0.7 %copy-start.2 = (s32[6,6,128]{2,1,0:T(8,128)S(1)}, s32[6,6,128]{2,1,0:T(8,128)}, u32[]{:S(2)}) copy-start(s32[6,6,128]{2,1,0:T(8,128)} %obstacle.1) | copy-start | bytes 55300
  9.1 5.3 %collective-permute-start.2 = (f32[80,128]{1,0:T(8,128)S(1)}, f32[80,128]{1,0:T(8,128)S(1)}, u32[]{:S(2)}, u32[]{:S(2)}) collective-permute-start(f32[80,128]{1,0:T(8,128)S(1)} %get-tuple-element.24), channel_id=1, source_target_pairs={{0,1},{1,2},{2,3},{3,4},{4,5},{5,6},{6,7},{7,0},{8,9},{9,10},{10,1... | collective-permute-start | bytes 122888 | tf_op jit(solution)/shard_map/ppermute | solution.py:605
  9.2 5.3 %collective-permute-start.3 = (f32[80,128]{1,0:T(8,128)S(1)}, f32[80,128]{1,0:T(8,128)S(1)}, u32[]{:S(2)}, u32[]{:S(2)}) collective-permute-start(f32[80,128]{1,0:T(8,128)S(1)} %get-tuple-element.25), channel_id=1, source_target_pairs={{0,7},{1,0},{2,1},{3,2},{4,3},{5,4},{6,5},{7,6},{8,15},{9,8},{10,9... | collective-permute-start | bytes 122888 | tf_op jit(solution)/shard_map/ppermute | solution.py:606

commit v3 on v2

--- a/solution.py
+++ b/solution.py
@@ -25,7 +25,7 @@
 LIMIT = 16 << 20
 
 LEV_BELOW, LEV_ROW, LEV_ABOVE = 0, 1, 2
-LEV_X_LOW, LEV_X_HIGH, LEV_OWN, LEV_Y_LOW, LEV_Y_HIGH = 3, 4, 5, 6, 7
+LEV_X_LOW, LEV_X_HIGH, LEV_OWN, LEV_Y_LOW, LEV_Y_HIGH, EVEN_SPAN = 3, 4, 5, 6, 7, 8
 
 X_FINE, X_MIDDLE = Q, Q + 9
 Y_SECOND, Y_THIRD, Y_CORNER = Q, 2 * Q, 2 * Q + 16
@@ -50,6 +50,11 @@
 def ring(axis, by):
     peers = lax.axis_size(axis)
     return [(i, (i + by) % peers) for i in range(peers)]
+
+
+def pairs(axis, odd):
+    peers = lax.axis_size(axis)
+    return [(i, (i + (1 if i % 2 == odd else -1)) % peers) for i in range(peers)]
 
 
 def roll_lane(v, by):
@@ -133,6 +138,8 @@
     for k, (r, c) in ((LEV_X_LOW, (0, 1)), (LEV_X_HIGH, (2, 1)), (LEV_OWN, (1, 1)), (LEV_Y_LOW, (1, 0)),
                       (LEV_Y_HIGH, (1, 2))):
         levels[k] = jnp.full((8, LANES), level[at_row[r], at_col[c]], I32)
+    even = lax.rem(col, 2) == 0 if n_col % 2 == 0 else True
+    levels[EVEN_SPAN] = jnp.full((8, LANES), jnp.where(even, 1, 0), I32)
     refined = levels[LEV_OWN] == 1
     for q in range(Q):
         s = jnp.full((8, LANES), rates[q], F32)
@@ -202,7 +209,7 @@
     return rows
 
 
-def pack_y_kernel(fine, coarse, from_low, from_high, levels, up, down, w_edge):
+def pack_y_kernel(fine, coarse, from_low, from_high, levels, first, second, w_edge, up, down):
     sy, cy, nzc = fine.shape[1], coarse.shape[1], coarse.shape[3]
     low_half = iota(1, (Q, LANES)) < nzc
     own = levels[LEV_OWN] == 1
@@ -228,6 +235,11 @@
         for k, q in enumerate(qs):
             at, n, s = fine_slot(k)
             out[at : at + n] = jnp.where(both[0:n], rows[q][s : s + n], out[at : at + n])
+    even = levels[EVEN_SPAN] == 1
+    for at in range(0, Y_ROWS, 8):
+        a, b = up[at : at + 8], down[at : at + 8]
+        first[at : at + 8] = jnp.where(even, a, b)
+        second[at : at + 8] = jnp.where(even, b, a)
 
 
 def forward(m0, m1, m2):
@@ -319,10 +331,10 @@
             out[k, t, q0 : q0 + n] = tile[x][:, 0:width]
 
 
-def coalesce(buf, t, out, at, thin):
+def coalesce(planes, out, at, thin):
     nzc = out.shape[3]
     for X in range(out.shape[0]):
-        s = (buf[2 * X, t] + buf[2 * X + 1, t]) + (buf[2 * X, t + 1] + buf[2 * X + 1, t + 1])
+        s = sum(p[2 * X] + p[2 * X + 1] for p in planes)
         out[X, at] = dot_exact(s, thin[...])[:, 0:nzc]
 
 
@@ -335,19 +347,20 @@
     store_rows(new, buf, at, range(1, cx + 1), nzc)
 
 
-def inner_kernel(fine, coarse, from_low, from_high, levels, coef, flags, c_wall, c_wide, refine, thin,
-                 out, c_out, w_in, ex_side, c_all, ghost, ex_mid, f_buf, c_buf, sems):
+def inner_kernel(fine, coarse, from_low, from_high, w_edge, levels, coef, flags, c_wall, c_wide, refine, thin,
+                 out, c_out, w_in, ex_side, c_all, f_in, aux, ghost, ex_mid, c_buf, sems):
     sx, sy, nz = fine.shape[0], fine.shape[1], fine.shape[3]
     cx, cy, nzc = coarse.shape[0], coarse.shape[1], coarse.shape[3]
     mid = sy // 2
     own = jnp.max(levels[LEV_OWN])
-    for side, msg in enumerate((from_low, from_high)):
-        v = dot_exact(msg[0:Q], refine[...])
-        ghost[side, 0, 0:Q] = v[:, 0:nz]
-        ghost[side, cy - 1, 0:Q] = v[:, nz : 2 * nz]
-        v = dot_exact(msg[X_MIDDLE : X_MIDDLE + 16], refine[...])
-        ghost[side, 1, 0:16] = v[:, 0:nz]
-        ghost[side, 1, 16:Q] = v[0 : Q - 16, nz : 2 * nz]
+    n = 8 * ((X_MIDDLE + 16 + 7) // 8)
+    both = dot_exact(jnp.concatenate([from_low[0:n], from_high[0:n]], axis=0), refine[...])
+    for side in range(2):
+        v = both[side * n : side * n + n]
+        ghost[side, 0, 0:Q] = v[0:Q, 0:nz]
+        ghost[side, cy - 1, 0:Q] = v[0:Q, nz : 2 * nz]
+        ghost[side, 1, 0:16] = v[X_MIDDLE : X_MIDDLE + 16, 0:nz]
+        ghost[side, 1, 16:Q] = v[X_MIDDLE : X_MIDDLE + Q - 16, nz : 2 * nz]
 
     def wide(J, I):
         if I == 0:
@@ -368,13 +381,14 @@
     def exploded(J, i):
         return ex_mid.at[i] if J == 2 else ex_side.at[J // 2, i]
 
-    copies = [pltpu.make_async_copy(f_buf.at[:, pl.ds(1, 2)], out.at[:, pl.ds(mid - 1, 2)], sems.at[0]),
+    copies = [pltpu.make_async_copy(f_in.at[:, pl.ds(mid - 2, 2)], out.at[:, pl.ds(mid - 1, 2)], sems.at[0]),
               pltpu.make_async_copy(c_buf, c_out.at[:, pl.ds(cy // 2, 1)], sems.at[1]),
-              pltpu.make_async_copy(f_buf, out.at[:, pl.ds(1, 4)], sems.at[0])]
+              pltpu.make_async_copy(f_in, out.at[:, pl.ds(1, sy - 2)], sems.at[0])]
 
     @pl.when(own == 1)
     def _():
         refined = (levels[LEV_X_LOW] == 1, levels[LEV_X_HIGH] == 1)
+        sub = iota(0)
         for y in range(1, sy - 1):
             a, b = pair_of(y + 1)
 
@@ -386,16 +400,27 @@
             rows = fine_plane(fine, from_low, from_high, y, mixed)
             for q in range(Q):
                 w_in[q, y - 1] = rows[q]
-        for y in (mid - 1, mid):
-            pulled = pull(lambda q: w_in[q, y - 1 - STEP[q][1]], lambda q: w_in[q, y - 1],
+
+        def plane(q, y):
+            if y in (0, sy - 1):
+                return w_edge[q, 0 if y == 0 else 1]
+            return w_in[q, y - 1]
+
+        for y in (mid - 1, mid, 1, sy - 2):
+            pulled = pull(lambda q: plane(q, y - STEP[q][1]), lambda q: plane(q, y),
                           bounce_mask(nz, wall_plane(flags, y, mid - 1)))
+            if y in (1, sy - 2):
+                for q in range(Q):
+                    aux[q, 0 if y == 1 else 1] = jnp.where(sub == 0, roll_sub(pulled[q], -1), roll_sub(pulled[q], 1))
             new = collide(pulled, coef)
-            stay = flags[y - mid + 1] == 1
-            new = [jnp.where(stay, w_in[q, y - 1], new[q]) for q in range(Q)]
-            store_rows(new, f_buf, y - 1, range(1, sx + 1), nz)
-        copies[0].start()
-        coalesce(f_buf, 1, c_buf, 0, thin)
-        copies[1].start()
+            if y in (mid - 1, mid):
+                stay = flags[y - mid + 1] == 1
+                new = [jnp.where(stay, w_in[q, y - 1], new[q]) for q in range(Q)]
+            store_rows(new, f_in, y - 1, range(1, sx + 1), nz)
+            if y == mid:
+                copies[0].start()
+                coalesce([f_in.at[:, mid - 2], f_in.at[:, mid - 1]], c_buf, 0, thin)
+                copies[1].start()
         copies[0].wait()
 
     @pl.when(own != 1)
@@ -403,7 +428,7 @@
         for y in range(1, sy - 1):
             a, b = pair_of(y + 1)
             for x in range(sx):
-                f_buf[x, y - 1] = blend(exploded(a, x + 1)[0:Q], exploded(b, x + 1)[0:Q])
+                f_in[x, y - 1] = blend(exploded(a, x + 1)[0:Q], exploded(b, x + 1)[0:Q])
         copies[2].start()
 
         def tile_of(Y):
@@ -430,36 +455,52 @@
     copies[1].wait()
 
 
-def outer_kernel(from_below, from_above, w_edge, w_in, c_all, ex_side, levels, coef, flags, c_wall, refine, thin,
-                 _out_in, _c_in, out, c_out, wide, ex_g, w_g, w_e, c_g, f_buf, c_buf, sems):
+def outer_kernel(first, second, w_edge, w_in, c_all, ex_side, f_in, aux, levels, coef, c_wall, refine, thin,
+                 _out_in, _c_in, out, c_out, msgs, wide, ex_g, w_g, w_e, c_g, f_buf, f_fix, s_buf, c_buf, sems):
     sx, sy, nz = out.shape[0], out.shape[1], out.shape[3]
     cx, cy, nzc = c_out.shape[0], c_out.shape[1], c_out.shape[3]
     own = jnp.max(levels[LEV_OWN])
     sub = iota(0)
-    for e, msg in enumerate((from_below, from_above)):
-        v = dot_exact(msg[0:72], refine[...])
-        wide[0, 0:Q] = v[0:Q, 0:nz]
-        wide[1, 0:Q] = v[0:Q, nz : 2 * nz]
-        wide[3, 0:Q] = v[Y_SECOND : Y_SECOND + Q, 0:nz]
-        wide[4, 0:Q] = v[Y_SECOND : Y_SECOND + Q, nz : 2 * nz]
-        wide[2, 0:16] = v[Y_THIRD : Y_THIRD + 16, 0:nz]
-        wide[2, 16:Q] = v[Y_THIRD : Y_THIRD + Q - 16, nz : 2 * nz]
+    even = levels[EVEN_SPAN] == 1
+    for at in range(0, Y_ROWS, 8):
+        a, b = first[at : at + 8], second[at : at + 8]
+        msgs[at : at + 8] = jnp.where(even, b, a)
+        msgs[Y_ROWS + at : Y_ROWS + at + 8] = jnp.where(even, a, b)
+    v = dot_exact(msgs[...], refine[...])
+    for e in range(2):
+        at = Y_ROWS * e
+        wide[0, 0:Q] = v[at : at + Q, 0:nz]
+        wide[1, 0:Q] = v[at : at + Q, nz : 2 * nz]
+        wide[3, 0:Q] = v[at + Y_SECOND : at + Y_SECOND + Q, 0:nz]
+        wide[4, 0:Q] = v[at + Y_SECOND : at + Y_SECOND + Q, nz : 2 * nz]
+        wide[2, 0:16] = v[at + Y_THIRD : at + Y_THIRD + 16, 0:nz]
+        wide[2, 16:Q] = v[at + Y_THIRD : at + Y_THIRD + Q - 16, nz : 2 * nz]
         for i in range(sx + 2):
             a, b = pair_of(i)
             ex_g[e, i] = blend(wide[a], wide[b])
 
-    def plane_copy(y):
-        return pltpu.make_async_copy(f_buf.at[:, pl.ds(y, 1)], out.at[:, pl.ds(y, 1)], sems.at[y])
+    def edge_copy(e):
+        y = (sy - 1) * e
+        return pltpu.make_async_copy(f_buf.at[:, pl.ds(e, 1)], out.at[:, pl.ds(y, 1)], sems.at[e])
 
     def coarse_copy(e):
-        return pltpu.make_async_copy(c_buf.at[:, pl.ds(e, 1)], c_out.at[:, pl.ds((cy - 1) * e, 1)],
-                                     sems.at[sy + e])
+        return pltpu.make_async_copy(c_buf.at[:, pl.ds(e, 1)], c_out.at[:, pl.ds((cy - 1) * e, 1)], sems.at[2 + e])
 
     @pl.when(own == 1)
     def _():
-        for e, msg in enumerate((from_below, from_above)):
+        ready = [pltpu.make_async_copy(f_in.at[pl.ds(1, sx - 2), pl.ds((sy - 3) * e, 1)],
+                                       out.at[pl.ds(1, sx - 2), pl.ds(1 + (sy - 3) * e, 1)], sems.at[4 + e])
+                 for e in range(2)]
+        fixed = [[pltpu.make_async_copy(f_fix.at[pl.ds(side, 1), pl.ds(e, 1)],
+                                        out.at[pl.ds((sx - 1) * side, 1), pl.ds(1 + (sy - 3) * e, 1)],
+                                        sems.at[6 + 2 * e + side]) for side in range(2)] for e in range(2)]
+        for c in ready:
+            c.start()
+        lane = iota(1)
+        inside = {0: None, 1: lane != 0, -1: lane != nz - 1}
+        for e in range(2):
+            msg = msgs.at[pl.ds(Y_ROWS * e, Y_ROWS)]
             qs = HIGH_Y if e == 0 else LOW_Y
-            ghost_j, edge_j = (0, 1) if e == 0 else (sy + 1, sy)
             far = levels[LEV_BELOW if e == 0 else LEV_ABOVE] == 1
             near = levels[LEV_Y_LOW if e == 0 else LEV_Y_HIGH] == 1
             for q0, n in OCTETS:
@@ -485,32 +526,56 @@
                     v = jnp.where(coarse_high, jnp.broadcast_to(v_high[q : q + 1], (8, LANES)), v)
                 w_e[q] = v
 
-            def plane(q, j):
-                if j == ghost_j:
-                    return w_g[qs.index(q)]
-                if j == edge_j:
-                    return w_e[q]
-                return w_in[q, j - 2]
-
-            for y in ((0, 1) if e == 0 else (sy - 1, sy - 2)):
-                pulled = pull(lambda q: plane(q, y + 1 - STEP[q][1]), lambda q: plane(q, y + 1),
-                              bounce_mask(nz, wall_plane(flags, y, sy // 2 - 1)))
-                store_rows(collide(pulled, coef), f_buf, y, range(1, sx + 1), nz)
-                plane_copy(y).start()
-            coalesce(f_buf, 0 if e == 0 else sy - 2, c_buf, e, thin)
+            def source(q):
+                return (w_g[qs.index(q)] if q in qs else
+                        w_e[q] if STEP[q][1] == 0 else w_in[q, (sy - 3) * e])
+
+            pulled = pull(source, lambda q: w_e[q], bounce_mask(nz, lambda ey: None))
+            spare = (sub == 0) | (sub == sx + 1)
+            for q in range(Q):
+                ex, _, ez = STEP[q]
+                v = aux[q, e]
+                if q in qs and ex != 0:
+                    m = sub == (0 if ex > 0 else sx + 1)
+                    if ez != 0:
+                        m = m & inside[ez]
+                    v = jnp.where(m, roll_lane(w_e[q], ez), v)
+                pulled[q] = jnp.where(spare, v, pulled[q])
+            new = collide(pulled, coef)
+            for q0, n in OCTETS:
+                tile = jnp.swapaxes(jnp.stack(new[q0 : q0 + n]), 0, 1)
+                for x in range(sx):
+                    f_buf[x, e, q0 : q0 + n] = tile[x + 1]
+                f_fix[0, e, q0 : q0 + n] = tile[0]
+                f_fix[1, e, q0 : q0 + n] = tile[sx + 1]
+            edge_copy(e).start()
+            for c in fixed[e]:
+                c.start()
+
+            def beside(x):
+                if x in (0, sx - 1):
+                    return f_fix[0 if x == 0 else 1, e]
+                return f_in[x, (sy - 3) * e]
+
+            for X in range(cx):
+                s_buf[QPAD * X : QPAD * X + Q] = ((f_buf[2 * X, e] + f_buf[2 * X + 1, e])
+                                                  + (beside(2 * X) + beside(2 * X + 1)))
+            mean = dot_exact(s_buf[...], thin[...])
+            for X in range(cx):
+                c_buf[X, e] = mean[QPAD * X : QPAD * X + Q, 0:nzc]
             coarse_copy(e).start()
-        plane_copy(1).wait()
-        plane_copy(sy - 2).wait()
+        for c in ready + fixed[0] + fixed[1]:
+            c.wait()
 
     @pl.when(own != 1)
     def _():
         wall = c_wall[...]
 
-        for e, msg in enumerate((from_below, from_above)):
-            y = 0 if e == 0 else sy - 1
+        for e in range(2):
+            msg = msgs.at[pl.ds(Y_ROWS * e, Y_ROWS)]
             for x in range(sx):
-                f_buf[x, y] = blend(ex_side[e, x + 1, 0:Q], ex_g[e, x + 1, 0:Q])
-            plane_copy(y).start()
+                f_buf[x, e] = blend(ex_side[e, x + 1, 0:Q], ex_g[e, x + 1, 0:Q])
+            edge_copy(e).start()
 
             def tile(I, q0, n):
                 at = Y_SECOND if I >= 3 else 0
@@ -535,9 +600,8 @@
             coarse_step(plane, 1 if e == 0 else cy, wall, coef, c_buf, e, nzc, cx, 2)
             coarse_copy(e).start()
 
-    plane_copy(0).wait()
-    plane_copy(sy - 1).wait()
     for e in range(2):
+        edge_copy(e).wait()
         coarse_copy(e).wait()
 
 
@@ -578,7 +642,7 @@
     levels, coef, flags, c_wall, c_wide, refine, thin = pl.pallas_call(
         tables_kernel,
         out_shape=(
-            struct((8, 8, LANES), I32),
+            struct((9, 8, LANES), I32),
             struct((Q + len(EVEN), 8, LANES)),
             struct((2, 8, LANES), I32),
             struct((8, LANES), I32),
@@ -594,19 +658,24 @@
     )(coarse, obstacle, block_level, relax_rates)
 
     y_message = struct((Y_ROWS, LANES))
-    up, down, w_edge = pl.pallas_call(
+    first, second, w_edge = pl.pallas_call(
         pack_y_kernel,
         out_shape=(y_message, y_message, struct((Q, 2, 8, LANES))),
         in_specs=[VMEM] * 5,
         out_specs=(VMEM,) * 3,
+        scratch_shapes=[pltpu.VMEM(y_message.shape, F32)] * 2,
         compiler_params=params(),
         name="pack_y",
     )(fine, coarse, from_low, from_high, levels)
-    from_below = lax.ppermute(up, "span", ring("span", 1))
-    from_above = lax.ppermute(down, "span", ring("span", -1))
+    if lax.axis_size("span") % 2 == 0:
+        second = lax.ppermute(second, "span", pairs("span", 1))
+        first = lax.ppermute(first, "span", pairs("span", 0))
+    else:
+        second, first = (lax.ppermute(first, "span", ring("span", 1)),
+                         lax.ppermute(second, "span", ring("span", -1)))
 
     fine_shape, coarse_shape = struct(fine.shape), struct(coarse.shape)
-    out, c_out, w_in, ex_side, c_all = pl.pallas_call(
+    out, c_out, w_in, ex_side, c_all, f_in, aux = pl.pallas_call(
         inner_kernel,
         out_shape=(
             fine_shape,
@@ -614,40 +683,44 @@
             struct((Q, sy - 2, 8, LANES)),
             struct((2, sx + 2, QPAD, nz)),
             struct((Q, cy, 8, LANES)),
+            struct((sx, sy - 2, Q, nz)),
+            struct((Q, 2, 8, LANES)),
         ),
-        in_specs=[VMEM] * 11,
-        out_specs=(ANY, ANY) + (VMEM,) * 3,
+        in_specs=[VMEM] * 12,
+        out_specs=(ANY, ANY) + (VMEM,) * 5,
         scratch_shapes=[
             pltpu.VMEM((2, cy, QPAD, nz), F32),
             pltpu.VMEM((sx + 2, QPAD, nz), F32),
-            pltpu.VMEM((sx, sy - 2, Q, nz), F32),
             pltpu.VMEM((cx, 1, Q, nzc), F32),
             pltpu.SemaphoreType.DMA((2,)),
         ],
         compiler_params=params(),
         cost_estimate=cost(20_000_000, 1_000_000),
         name="inner",
-    )(fine, coarse, from_low, from_high, levels, coef, flags, c_wall, c_wide, refine, thin)
+    )(fine, coarse, from_low, from_high, w_edge, levels, coef, flags, c_wall, c_wide, refine, thin)
 
     out, c_out = pl.pallas_call(
         outer_kernel,
         out_shape=(fine_shape, coarse_shape),
-        in_specs=[VMEM] * 12 + [ANY, ANY],
+        in_specs=[VMEM] * 13 + [ANY, ANY],
         out_specs=(ANY, ANY),
         scratch_shapes=[
+            pltpu.VMEM((2 * Y_ROWS, LANES), F32),
             pltpu.VMEM((5, QPAD, nz), F32),
             pltpu.VMEM((2, sx + 2, QPAD, nz), F32),
             pltpu.VMEM((9, 8, LANES), F32),
             pltpu.VMEM((Q, 8, LANES), F32),
             pltpu.VMEM((Q, 2, 8, LANES), F32),
-            pltpu.VMEM((sx, sy, Q, nz), F32),
+            pltpu.VMEM((sx, 2, Q, nz), F32),
+            pltpu.VMEM((2, 2, Q, nz), F32),
+            pltpu.VMEM((QPAD * cx, nz), F32),
             pltpu.VMEM((cx, 2, Q, nzc), F32),
-            pltpu.SemaphoreType.DMA((sy + 2,)),
+            pltpu.SemaphoreType.DMA((10,)),
         ],
-        input_output_aliases={12: 0, 13: 1},
+        input_output_aliases={13: 0, 14: 1},
         compiler_params=params(),
         name="outer",
-    )(from_below, from_above, w_edge, w_in, c_all, ex_side, levels, coef, flags, c_wall, refine, thin,
+    )(first, second, w_edge, w_in, c_all, ex_side, f_in, aux, levels, coef, c_wall, refine, thin,
       out, c_out)
     return jnp.transpose(out, (2, 0, 1, 3)), jnp.transpose(c_out, (2, 0, 1, 3))
 

time: 16.2 us -> 16.4 us (1.012); the launches traced: 16.2 us -> 16.2 us
  Pallas kernels: 5.4 us -> 5.19 us
  starting transfers between devices: 7.63 us -> 7.83 us
    pallas_call x1, Pallas kernels: 1.75 us -> 1.49 us  [local(): pl.pallas_call(outer_kernel, out_shape=(fine_shape, coarse_shape), in_spe...]
    ppermute x2, starting transfers between devices: 3.59 us -> 3.78 us  [the longest x1 3.71 us: local(): second = lax.ppermute(second, 'span', pairs('span', 1))]
  transfers between devices with their start and end apart: 4 -> 4, of which waited for: 3 -> 3; matrix products, arithmetic and copies ran while one was open for 0% -> 0% of each run, Pallas kernels for 14% -> 15%
where the time goes in v3:
time: 16.4 us; the launch traced here: 16.2 us
  starting transfers between devices  7.83 us (48%)
  Pallas kernels  5.19 us (32%)
  waiting for transfers between devices  1.68 us (10%)
  local copies, waits for them, and re-layouts  0.75 us (5%)
  between operations  0.71 us (4%)
    ppermute x1, starting transfers between devices, local(): second = lax.ppermute(second, 'span', pairs('span', 1))  3.71 us
    ppermute x1, starting transfers between devices, local(): from_low = lax.ppermute(up, 'stream', ring('stream', 1))  3.01 us
    pallas_call x1, Pallas kernels, local(): pl.pallas_call(outer_kernel, out_shape=(fine_shape, coarse_shape), in_spe...  1.49 us
    pallas_call x1, Pallas kernels, local(): pl.pallas_call(inner_kernel, out_shape=(fine_shape, coarse_shape, struct(...  1.48 us
    pallas_call x1, Pallas kernels, local(): pl.pallas_call(pack_x_kernel, out_shape=(x_message, x_message), in_specs=...  1.24 us
    ppermute x1, waiting for transfers between devices, local(): from_high = lax.ppermute(down, 'stream', ring('stream', -1))  1.06 us
    ppermute x1, starting transfers between devices, local(): from_high = lax.ppermute(down, 'stream', ring('stream', -1))  1.03 us
    pallas_call x1, Pallas kernels, local(): pl.pallas_call(tables_kernel, out_shape=(struct((9, 8, LANES), I32), stru...  0.88 us
  transfers between devices with their start and end apart: 4, of which 3 were waited for; matrix products, arithmetic and copies ran while one was open for 0% of the time, Pallas kernels for 15%

profile of v3, /device:TPU:0, one launch (start us, length us, event | category | flops | bytes accessed | tf_op | source)
XLA Modules:
  0.0 16.2 jit_solution(17970715338716656802)
XLA Ops:
  0.6 0.0 copy-start
  0.6 0.0 copy-start.1
  0.6 1.2 %pack_x.1 = (f32[88,128]{1,0:T(8,128)S(1)}, f32[88,128]{1,0:T(8,128)S(1)}) custom-call(f32[6,6,27,128]{3,2,1,0:T(8,128)} %bitcast.4, f32[3,3,27,64]{3,2,1,0:T(8,128)} %bitcast.7, s32[4,8]{1,0:T(4,128)} %level.3), custom_call_target="tpu_custom_call" | custom-call | tf_op jit(solution)/shard_map/pack_x/pallas_call | solution.py:623
  1.9 0.0 copy-start.3
  1.9 0.0 copy-start.4
  1.9 3.0 %collective-permute-start = (f32[88,128]{1,0:T(8,128)S(1)}, f32[88,128]{1,0:T(8,128)S(1)}, u32[]{:S(2)}, u32[]{:S(2)}) collective-permute-start(f32[88,128]{1,0:T(8,128)S(1)} %get-tuple-element.23), channel_id=1, source_target_pairs={{0,8},{8,16},{16,24},{24,0},{1,9},{9,17},{17,25},{25,1},{2,10},{10... | collective-permute-start | bytes 135176 | tf_op jit(solution)/shard_map/ppermute | solution.py:639
  4.9 1.0 %collective-permute-start.1 = (f32[88,128]{1,0:T(8,128)S(1)}, f32[88,128]{1,0:T(8,128)S(1)}, u32[]{:S(2)}, u32[]{:S(2)}) collective-permute-start(f32[88,128]{1,0:T(8,128)S(1)} %get-tuple-element.24), channel_id=1, source_target_pairs={{0,24},{8,0},{16,8},{24,16},{1,25},{9,1},{17,9},{25,17},{2,26},{10... | collective-permute-start | bytes 135176 | tf_op jit(solution)/shard_map/ppermute | solution.py:640
  6.0 0.0 copy-done.1
  6.0 0.0 copy-done.3
  6.0 0.0 copy-done.4
  6.0 0.0 copy-start.2
  6.0 0.7 %copy-done.2 = s32[6,6,128]{2,1,0:T(8,128)S(1)} copy-done((s32[6,6,128]{2,1,0:T(8,128)S(1)}, s32[6,6,128]{2,1,0:T(8,128)}, u32[]{:S(2)}) %copy-start.2) | copy-done | bytes 18456
  6.7 0.9 %tables.1 = (s32[9,8,128]{2,1,0:T(8,128)S(1)}, f32[35,8,128]{2,1,0:T(8,128)S(1)}, s32[2,8,128]{2,1,0:T(8,128)S(1)}, s32[8,128]{1,0:T(8,128)S(1)}, f32[3,3,32,128...) custom-call(f32[3,3,27,64]{3,2,1,0:T(8,128)S(1)} %bitcast.8, ...), custom_call_target="tpu_custom_call" | custom-call | flops 10000000 | bytes 1000000 | tf_op jit(solution)/shard_map/tables/pallas_call | solution.py:642
  7.6 0.3 %collective-permute-done.from_low = f32[88,128]{1,0:T(8,128)S(1)} collective-permute-done((f32[88,128]{1,0:T(8,128)S(1)}, f32[88,128]{1,0:T(8,128)S(1)}, u32[]{:S(2)}, u32[]{:S(2)}) %collective-permute-start) | collective-permute-done | bytes 45088 | tf_op jit(solution)/shard_map/ppermute | solution.py:639
  7.9 1.1 %collective-permute-done.1.from_high = f32[88,128]{1,0:T(8,128)S(1)} collective-permute-done((f32[88,128]{1,0:T(8,128)S(1)}, f32[88,128]{1,0:T(8,128)S(1)}, u32[]{:S(2)}, u32[]{:S(2)}) %collective-permute-start.1) | collective-permute-done | bytes 45088 | tf_op jit(solution)/shard_map/ppermute | solution.py:640
  9.0 0.0 copy-done
  9.0 0.1 pack_y.1
  9.1 0.1 collective-permute-start.2
  9.2 3.7 %collective-permute-start.3 = (f32[80,128]{1,0:T(8,128)S(1)}, f32[80,128]{1,0:T(8,128)S(1)}, u32[]{:S(2)}, u32[]{:S(2)}) collective-permute-start(f32[80,128]{1,0:T(8,128)S(1)} %get-tuple-element.27), channel_id=1, source_target_pairs={{0,7},{1,2},{2,1},{3,4},{4,3},{5,6},{6,5},{7,0},{8,15},{9,10},{10,... | collective-permute-start | bytes 122888 | tf_op jit(solution)/shard_map/ppermute | solution.py:671
  12.9 1.5 %inner.1 = (f32[6,6,27,128]{3,2,1,0:T(8,128)}, f32[3,3,27,64]{3,2,1,0:T(8,128)}, f32[27,4,8,128]{3,2,1,0:T(8,128)S(1)}, f32[2,8,32,128]{3,2,1,0:T(8,128)S(1)}, f...) custom-call(f32[6,6,27,128]{3,2,1,0:T(8,128)S(1)} %bitcast.6, ...), custom_call_target="tpu_custom_call" | custom-call | flops 20000000 | bytes 1000000 | tf_op jit(solution)/shard_map/inner/pallas_call | solution.py:678
  14.4 0.0 collective-permute-done.2.first
  14.4 0.3 %collective-permute-done.3.second = f32[80,128]{1,0:T(8,128)S(1)} collective-permute-done((f32[80,128]{1,0:T(8,128)S(1)}, f32[80,128]{1,0:T(8,128)S(1)}, u32[]{:S(2)}, u32[]{:S(2)}) %collective-permute-start.3) | collective-permute-done | bytes 40992 | tf_op jit(solution)/shard_map/ppermute | solution.py:671
  14.7 1.5 %outer.1 = (f32[6,6,27,128]{3,2,1,0:T(8,128)}, f32[3,3,27,64]{3,2,1,0:T(8,128)}) custom-call(f32[80,128]{1,0:T(8,128)S(1)} %collective-permute-done.2.first, f32[80,128]{1,0:T(8,128)S(1)} %collective-permute-done.3.second, f32[27,2,8,128]{3,2,1,0:T(8,128)S(1)} %get-tuple-element.28.w_edge, ...), custom_call_target="tpu_custom_call", output_to_operand_aliasing={{0}: (13, {}), {1}: (14, {})} | custom-call | tf_op jit(solution)/shard_map/outer/pallas_call | solution.py:702
Async XLA Ops:
  0.6 8.4 %copy-start = (f32[27,6,6,128]{3,0,2,1:T(8,128)S(1)}, f32[27,6,6,128]{3,0,2,1:T(8,128)}, u32[]{:S(2)}) copy-start(f32[27,6,6,128]{3,0,2,1:T(8,128)} %param.5) | copy-start | bytes 1492996
  0.6 5.3 %copy-start.1 = (f32[27,3,3,64]{3,0,2,1:T(8,128)S(1)}, f32[27,3,3,64]{3,0,2,1:T(8,128)}, u32[]{:S(2)}) copy-start(f32[27,3,3,64]{3,0,2,1:T(8,128)} %param.6) | copy-start | bytes 186628
  1.9 4.1 %copy-start.3 = (s32[4,8]{1,0:T(4,128)S(1)}, s32[4,8]{1,0:T(4,128)}, u32[]{:S(2)}) copy-start(s32[4,8]{1,0:T(4,128)} %level.3) | copy-start | bytes 388
  1.9 4.1 %copy-start.4 = (f32[27]{0:T(128)S(1)}, f32[27]{0:T(128)}, u32[]{:S(2)}) copy-start(f32[27]{0:T(128)} %rates.1) | copy-start | bytes 328
  1.9 6.0 %collective-permute-start = (f32[88,128]{1,0:T(8,128)S(1)}, f32[88,128]{1,0:T(8,128)S(1)}, u32[]{:S(2)}, u32[]{:S(2)}) collective-permute-start(f32[88,128]{1,0:T(8,128)S(1)} %get-tuple-element.23), channel_id=1, source_target_pairs={{0,8},{8,16},{16,24},{24,0},{1,9},{9,17},{17,25},{25,1},{2,10},{10... | collective-permute-start | bytes 135176 | tf_op jit(solution)/shard_map/ppermute | solution.py:639
  4.9 4.0 %collective-permute-start.1 = (f32[88,128]{1,0:T(8,128)S(1)}, f32[88,128]{1,0:T(8,128)S(1)}, u32[]{:S(2)}, u32[]{:S(2)}) collective-permute-start(f32[88,128]{1,0:T(8,128)S(1)} %get-tuple-element.24), channel_id=1, source_target_pairs={{0,24},{8,0},{16,8},{24,16},{1,25},{9,1},{17,9},{25,17},{2,26},{10... | collective-permute-start | bytes 135176 | tf_op jit(solution)/shard_map/ppermute | solution.py:640
  6.0 0.7 %copy-start.2 = (s32[6,6,128]{2,1,0:T(8,128)S(1)}, s32[6,6,128]{2,1,0:T(8,128)}, u32[]{:S(2)}) copy-start(s32[6,6,128]{2,1,0:T(8,128)} %obstacle.1) | copy-start | bytes 55300
  9.1 5.3 %collective-permute-start.2 = (f32[80,128]{1,0:T(8,128)S(1)}, f32[80,128]{1,0:T(8,128)S(1)}, u32[]{:S(2)}, u32[]{:S(2)}) collective-permute-start(f32[80,128]{1,0:T(8,128)S(1)} %get-tuple-element.26), channel_id=1, source_target_pairs={{0,1},{1,0},{2,3},{3,2},{4,5},{5,4},{6,7},{7,6},{8,9},{9,8},{10,11... | collective-permute-start | bytes 122888 | tf_op jit(solution)/shard_map/ppermute | solution.py:672
  9.2 5.5 %collective-permute-start.3 = (f32[80,128]{1,0:T(8,128)S(1)}, f32[80,128]{1,0:T(8,128)S(1)}, u32[]{:S(2)}, u32[]{:S(2)}) collective-permute-start(f32[80,128]{1,0:T(8,128)S(1)} %get-tuple-element.27), channel_id=1, source_target_pairs={{0,7},{1,2},{2,1},{3,4},{4,3},{5,6},{6,5},{7,0},{8,15},{9,10},{10,... | collective-permute-start | bytes 122888 | tf_op jit(solution)/shard_map/ppermute | solution.py:671

commit v4 on v3

--- a/solution.py
+++ b/solution.py
@@ -209,7 +209,7 @@
     return rows
 
 
-def pack_y_kernel(fine, coarse, from_low, from_high, levels, first, second, w_edge, up, down):
+def pack_y_kernel(fine, coarse, from_low, from_high, levels, second, first, w_edge, up, down):
     sy, cy, nzc = fine.shape[1], coarse.shape[1], coarse.shape[3]
     low_half = iota(1, (Q, LANES)) < nzc
     own = levels[LEV_OWN] == 1
@@ -455,7 +455,7 @@
     copies[1].wait()
 
 
-def outer_kernel(first, second, w_edge, w_in, c_all, ex_side, f_in, aux, levels, coef, c_wall, refine, thin,
+def outer_kernel(second, first, w_edge, w_in, c_all, ex_side, f_in, aux, levels, coef, c_wall, refine, thin,
                  _out_in, _c_in, out, c_out, msgs, wide, ex_g, w_g, w_e, c_g, f_buf, f_fix, s_buf, c_buf, sems):
     sx, sy, nz = out.shape[0], out.shape[1], out.shape[3]
     cx, cy, nzc = c_out.shape[0], c_out.shape[1], c_out.shape[3]
@@ -658,7 +658,7 @@
     )(coarse, obstacle, block_level, relax_rates)
 
     y_message = struct((Y_ROWS, LANES))
-    first, second, w_edge = pl.pallas_call(
+    second, first, w_edge = pl.pallas_call(
         pack_y_kernel,
         out_shape=(y_message, y_message, struct((Q, 2, 8, LANES))),
         in_specs=[VMEM] * 5,
@@ -720,7 +720,7 @@
         input_output_aliases={13: 0, 14: 1},
         compiler_params=params(),
         name="outer",
-    )(first, second, w_edge, w_in, c_all, ex_side, f_in, aux, levels, coef, c_wall, refine, thin,
+    )(second, first, w_edge, w_in, c_all, ex_side, f_in, aux, levels, coef, c_wall, refine, thin,
       out, c_out)
     return jnp.transpose(out, (2, 0, 1, 3)), jnp.transpose(c_out, (2, 0, 1, 3))
 

time: 16.4 us -> 16 us (0.976)
  waiting for transfers between devices: 1.68 us -> 3.67 us
  starting transfers between devices: 7.83 us -> 5.95 us
  Pallas kernels: 5.19 us -> 4.77 us
    ppermute x1, waiting for transfers between devices: 0.29 us -> 2.28 us  [local(): second = lax.ppermute(second, 'span', pairs('span', 1))]
    ppermute x1, starting transfers between devices: 3.71 us -> 1.9 us  [local(): second = lax.ppermute(second, 'span', pairs('span', 1))]
    pallas_call x1, Pallas kernels: 1.48 us -> 1.18 us  [local(): pl.pallas_call(inner_kernel, out_shape=(fine_shape, coarse_shape, struct(...]
  transfers between devices with their start and end apart: 4 -> 4, of which waited for: 3 -> 3; matrix products, arithmetic and copies ran while one was open for 0% -> 0% of each run, Pallas kernels for 15% -> 13%
where the time goes in v4:
time: 16 us; the launch traced here: 15.8 us
  starting transfers between devices  5.95 us (37%)
  Pallas kernels  4.77 us (30%)
  waiting for transfers between devices  3.67 us (23%)
  local copies, waits for them, and re-layouts  0.75 us (5%)
  between operations  0.69 us (4%)
    ppermute x1, starting transfers between devices, local(): from_low = lax.ppermute(up, 'stream', ring('stream', 1))  3.02 us
    ppermute x1, waiting for transfers between devices, local(): second = lax.ppermute(second, 'span', pairs('span', 1))  2.28 us
    ppermute x1, starting transfers between devices, local(): second = lax.ppermute(second, 'span', pairs('span', 1))  1.9 us
    pallas_call x1, Pallas kernels, local(): pl.pallas_call(outer_kernel, out_shape=(fine_shape, coarse_shape), in_spe...  1.36 us
    pallas_call x1, Pallas kernels, local(): pl.pallas_call(pack_x_kernel, out_shape=(x_message, x_message), in_specs=...  1.24 us
    pallas_call x1, Pallas kernels, local(): pl.pallas_call(inner_kernel, out_shape=(fine_shape, coarse_shape, struct(...  1.18 us
    ppermute x1, waiting for transfers between devices, local(): from_high = lax.ppermute(down, 'stream', ring('stream', -1))  1.06 us
    ppermute x1, starting transfers between devices, local(): from_high = lax.ppermute(down, 'stream', ring('stream', -1))  1.02 us
  transfers between devices with their start and end apart: 4, of which 3 were waited for; matrix products, arithmetic and copies ran while one was open for 0% of the time, Pallas kernels for 13%

profile of v4, /device:TPU:0, one launch (start us, length us, event | category | flops | bytes accessed | tf_op | source)
XLA Modules:
  0.0 15.8 jit_solution(11594317531527673562)
XLA Ops:
  0.6 0.0 copy-start
  0.6 0.0 copy-start.1
  0.6 1.2 %pack_x.1 = (f32[88,128]{1,0:T(8,128)S(1)}, f32[88,128]{1,0:T(8,128)S(1)}) custom-call(f32[6,6,27,128]{3,2,1,0:T(8,128)} %bitcast.4, f32[3,3,27,64]{3,2,1,0:T(8,128)} %bitcast.7, s32[4,8]{1,0:T(4,128)} %level.3), custom_call_target="tpu_custom_call" | custom-call | tf_op jit(solution)/shard_map/pack_x/pallas_call | solution.py:623
  1.9 0.0 copy-start.3
  1.9 0.0 copy-start.4
  1.9 3.0 %collective-permute-start = (f32[88,128]{1,0:T(8,128)S(1)}, f32[88,128]{1,0:T(8,128)S(1)}, u32[]{:S(2)}, u32[]{:S(2)}) collective-permute-start(f32[88,128]{1,0:T(8,128)S(1)} %get-tuple-element.23), channel_id=1, source_target_pairs={{0,8},{8,16},{16,24},{24,0},{1,9},{9,17},{17,25},{25,1},{2,10},{10... | collective-permute-start | bytes 135176 | tf_op jit(solution)/shard_map/ppermute | solution.py:639
  4.9 1.0 %collective-permute-start.1 = (f32[88,128]{1,0:T(8,128)S(1)}, f32[88,128]{1,0:T(8,128)S(1)}, u32[]{:S(2)}, u32[]{:S(2)}) collective-permute-start(f32[88,128]{1,0:T(8,128)S(1)} %get-tuple-element.24), channel_id=1, source_target_pairs={{0,24},{8,0},{16,8},{24,16},{1,25},{9,1},{17,9},{25,17},{2,26},{10... | collective-permute-start | bytes 135176 | tf_op jit(solution)/shard_map/ppermute | solution.py:640
  6.0 0.0 copy-done.1
  6.0 0.0 copy-done.3
  6.0 0.0 copy-done.4
  6.0 0.0 copy-start.2
  6.0 0.7 %copy-done.2 = s32[6,6,128]{2,1,0:T(8,128)S(1)} copy-done((s32[6,6,128]{2,1,0:T(8,128)S(1)}, s32[6,6,128]{2,1,0:T(8,128)}, u32[]{:S(2)}) %copy-start.2) | copy-done | bytes 18456
  6.7 0.9 %tables.1 = (s32[9,8,128]{2,1,0:T(8,128)S(1)}, f32[35,8,128]{2,1,0:T(8,128)S(1)}, s32[2,8,128]{2,1,0:T(8,128)S(1)}, s32[8,128]{1,0:T(8,128)S(1)}, f32[3,3,32,128...) custom-call(f32[3,3,27,64]{3,2,1,0:T(8,128)S(1)} %bitcast.8, ...), custom_call_target="tpu_custom_call" | custom-call | flops 10000000 | bytes 1000000 | tf_op jit(solution)/shard_map/tables/pallas_call | solution.py:642
  7.6 0.3 %collective-permute-done.from_low = f32[88,128]{1,0:T(8,128)S(1)} collective-permute-done((f32[88,128]{1,0:T(8,128)S(1)}, f32[88,128]{1,0:T(8,128)S(1)}, u32[]{:S(2)}, u32[]{:S(2)}) %collective-permute-start) | collective-permute-done | bytes 45088 | tf_op jit(solution)/shard_map/ppermute | solution.py:639
  7.9 1.1 %collective-permute-done.1.from_high = f32[88,128]{1,0:T(8,128)S(1)} collective-permute-done((f32[88,128]{1,0:T(8,128)S(1)}, f32[88,128]{1,0:T(8,128)S(1)}, u32[]{:S(2)}, u32[]{:S(2)}) %collective-permute-start.1) | collective-permute-done | bytes 45088 | tf_op jit(solution)/shard_map/ppermute | solution.py:640
  9.0 0.0 copy-done
  9.0 0.1 pack_y.1
  9.1 1.9 %collective-permute-start.2 = (f32[80,128]{1,0:T(8,128)S(1)}, f32[80,128]{1,0:T(8,128)S(1)}, u32[]{:S(2)}, u32[]{:S(2)}) collective-permute-start(f32[80,128]{1,0:T(8,128)S(1)} %get-tuple-element.26), channel_id=1, source_target_pairs={{0,7},{1,2},{2,1},{3,4},{4,3},{5,6},{6,5},{7,0},{8,15},{9,10},{10,... | collective-permute-start | bytes 122888 | tf_op jit(solution)/shard_map/ppermute | solution.py:671
  11.0 0.0 collective-permute-start.3
  11.0 1.2 %inner.1 = (f32[6,6,27,128]{3,2,1,0:T(8,128)}, f32[3,3,27,64]{3,2,1,0:T(8,128)}, f32[27,4,8,128]{3,2,1,0:T(8,128)S(1)}, f32[2,8,32,128]{3,2,1,0:T(8,128)S(1)}, f...) custom-call(f32[6,6,27,128]{3,2,1,0:T(8,128)S(1)} %bitcast.6, ...), custom_call_target="tpu_custom_call" | custom-call | flops 20000000 | bytes 1000000 | tf_op jit(solution)/shard_map/inner/pallas_call | solution.py:678
  12.2 2.3 %collective-permute-done.2.second = f32[80,128]{1,0:T(8,128)S(1)} collective-permute-done((f32[80,128]{1,0:T(8,128)S(1)}, f32[80,128]{1,0:T(8,128)S(1)}, u32[]{:S(2)}, u32[]{:S(2)}) %collective-permute-start.2) | collective-permute-done | bytes 40992 | tf_op jit(solution)/shard_map/ppermute | solution.py:671
  14.5 0.0 collective-permute-done.3.first
  14.5 1.4 %outer.1 = (f32[6,6,27,128]{3,2,1,0:T(8,128)}, f32[3,3,27,64]{3,2,1,0:T(8,128)}) custom-call(f32[80,128]{1,0:T(8,128)S(1)} %collective-permute-done.2.second, f32[80,128]{1,0:T(8,128)S(1)} %collective-permute-done.3.first, f32[27,2,8,128]{3,2,1,0:T(8,128)S(1)} %get-tuple-element.28.w_edge, ...), custom_call_target="tpu_custom_call", output_to_operand_aliasing={{0}: (13, {}), {1}: (14, {})} | custom-call | tf_op jit(solution)/shard_map/outer/pallas_call | solution.py:702
Async XLA Ops:
  0.6 8.4 %copy-start = (f32[27,6,6,128]{3,0,2,1:T(8,128)S(1)}, f32[27,6,6,128]{3,0,2,1:T(8,128)}, u32[]{:S(2)}) copy-start(f32[27,6,6,128]{3,0,2,1:T(8,128)} %param.5) | copy-start | bytes 1492996
  0.6 5.3 %copy-start.1 = (f32[27,3,3,64]{3,0,2,1:T(8,128)S(1)}, f32[27,3,3,64]{3,0,2,1:T(8,128)}, u32[]{:S(2)}) copy-start(f32[27,3,3,64]{3,0,2,1:T(8,128)} %param.6) | copy-start | bytes 186628
  1.9 4.1 %copy-start.3 = (s32[4,8]{1,0:T(4,128)S(1)}, s32[4,8]{1,0:T(4,128)}, u32[]{:S(2)}) copy-start(s32[4,8]{1,0:T(4,128)} %level.3) | copy-start | bytes 388
  1.9 4.1 %copy-start.4 = (f32[27]{0:T(128)S(1)}, f32[27]{0:T(128)}, u32[]{:S(2)}) copy-start(f32[27]{0:T(128)} %rates.1) | copy-start | bytes 328
  1.9 6.0 %collective-permute-start = (f32[88,128]{1,0:T(8,128)S(1)}, f32[88,128]{1,0:T(8,128)S(1)}, u32[]{:S(2)}, u32[]{:S(2)}) collective-permute-start(f32[88,128]{1,0:T(8,128)S(1)} %get-tuple-element.23), channel_id=1, source_target_pairs={{0,8},{8,16},{16,24},{24,0},{1,9},{9,17},{17,25},{25,1},{2,10},{10... | collective-permute-start | bytes 135176 | tf_op jit(solution)/shard_map/ppermute | solution.py:639
  4.9 4.0 %collective-permute-start.1 = (f32[88,128]{1,0:T(8,128)S(1)}, f32[88,128]{1,0:T(8,128)S(1)}, u32[]{:S(2)}, u32[]{:S(2)}) collective-permute-start(f32[88,128]{1,0:T(8,128)S(1)} %get-tuple-element.24), channel_id=1, source_target_pairs={{0,24},{8,0},{16,8},{24,16},{1,25},{9,1},{17,9},{25,17},{2,26},{10... | collective-permute-start | bytes 135176 | tf_op jit(solution)/shard_map/ppermute | solution.py:640
  6.0 0.7 %copy-start.2 = (s32[6,6,128]{2,1,0:T(8,128)S(1)}, s32[6,6,128]{2,1,0:T(8,128)}, u32[]{:S(2)}) copy-start(s32[6,6,128]{2,1,0:T(8,128)} %obstacle.1) | copy-start | bytes 55300
  9.1 5.4 %collective-permute-start.2 = (f32[80,128]{1,0:T(8,128)S(1)}, f32[80,128]{1,0:T(8,128)S(1)}, u32[]{:S(2)}, u32[]{:S(2)}) collective-permute-start(f32[80,128]{1,0:T(8,128)S(1)} %get-tuple-element.26), channel_id=1, source_target_pairs={{0,7},{1,2},{2,1},{3,4},{4,3},{5,6},{6,5},{7,0},{8,15},{9,10},{10,... | collective-permute-start | bytes 122888 | tf_op jit(solution)/shard_map/ppermute | solution.py:671
  11.0 3.5 %collective-permute-start.3 = (f32[80,128]{1,0:T(8,128)S(1)}, f32[80,128]{1,0:T(8,128)S(1)}, u32[]{:S(2)}, u32[]{:S(2)}) collective-permute-start(f32[80,128]{1,0:T(8,128)S(1)} %get-tuple-element.27), channel_id=1, source_target_pairs={{0,1},{1,0},{2,3},{3,2},{4,5},{5,4},{6,7},{7,6},{8,9},{9,8},{10,11... | collective-permute-start | bytes 122888 | tf_op jit(solution)/shard_map/ppermute | solution.py:672

commit v5 on v4

--- a/solution.py
+++ b/solution.py
@@ -73,12 +73,16 @@
     return jnp.broadcast_to(ref[at : at + 1], (8, LANES))
 
 
+def dot_parts(x, m, count):
+    parts = []
+    for _ in range(count):
+        parts.append(x.astype(BF16))
+        x = x - parts[-1].astype(F32)
+    return sum(jnp.dot(p, m, preferred_element_type=F32) for p in reversed(parts))
+
+
 def dot_exact(x, m):
-    high = x.astype(BF16)
-    rest = x - high.astype(F32)
-    middle = rest.astype(BF16)
-    low = (rest - middle.astype(F32)).astype(BF16)
-    return sum(jnp.dot(p, m, preferred_element_type=F32) for p in (low, middle, high))
+    return dot_parts(x, m, 3)
 
 
 def pair_of(i):
@@ -90,33 +94,35 @@
     return 0.75 * a + 0.25 * b
 
 
-def pack_x_kernel(fine, coarse, level, up, down, f_low, f_high, c_low, c_high, lev, sems):
+def pack_x_kernel(fine, coarse, level, up, down, f_low, f_high, c_low, c_high, middle, lev, sems):
     sx, sy, cx = fine.shape[0], fine.shape[1], coarse.shape[0]
+    fetch_level = pltpu.make_async_copy(level, lev, sems.at[4])
     copies = [
-        pltpu.make_async_copy(level, lev, sems.at[4]),
-        pltpu.make_async_copy(fine.at[sx - 1], f_high, sems.at[0]),
+        pltpu.make_async_copy(fine.at[sx - 1, :, pl.ds(16, Q - 16)], f_high, sems.at[0]),
         pltpu.make_async_copy(coarse.at[cx - 1], c_high, sems.at[1]),
-        pltpu.make_async_copy(fine.at[0], f_low, sems.at[2]),
+        pltpu.make_async_copy(fine.at[0, :, pl.ds(0, 16)], f_low, sems.at[2]),
         pltpu.make_async_copy(coarse.at[0], c_low, sems.at[3]),
     ]
+    fetch_level.start()
     for c in copies:
         c.start()
     for c in copies:
         c.wait()
     cy, nzc = c_low.shape[0], c_low.shape[2]
-    n_row = lev.shape[0]
-    row, col = lax.axis_index("stream"), lax.axis_index("span")
-    own = lev[row, col]
-    for out, f, c, qs, to in ((up, f_high, c_high, HIGH_X, row + 1), (down, f_low, c_low, LOW_X, row + n_row - 1)):
+    for k, (out, f, c, q0) in enumerate(((up, f_high, c_high, HIGH_X[0] - 16), (down, f_low, c_low, LOW_X[0]))):
+        middle[k, :, 0:nzc] = c[1, 0:16]
+        middle[k, 0 : Q - 16, nzc : 2 * nzc] = c[1, 16:Q]
         out[0:Q, 0:nzc] = c[0]
         out[0:Q, nzc : 2 * nzc] = c[cy - 1]
         for y in range(sy):
-            out[X_FINE + 9 * y : X_FINE + 9 * y + 9] = f[y, qs[0] : qs[0] + 9]
-
-        @pl.when((own != 1) | (lev[lax.rem(to, n_row), col] != 1))
-        def _(out=out, c=c):
-            out[X_MIDDLE : X_MIDDLE + 16, 0:nzc] = c[1, 0:16]
-            out[X_MIDDLE : X_MIDDLE + Q - 16, nzc : 2 * nzc] = c[1, 16:Q]
+            out[X_FINE + 9 * y : X_FINE + 9 * y + 9] = f[y, q0 : q0 + 9]
+    fetch_level.wait()
+    n_row = lev.shape[0]
+    row, col = lax.axis_index("stream"), lax.axis_index("span")
+    for k, (out, to) in enumerate(((up, row + 1), (down, row + n_row - 1))):
+        both = lev[row, col] * lev[lax.rem(to, n_row), col]
+        at = slice(X_MIDDLE, X_MIDDLE + 16)
+        out[at] = jnp.where(jnp.full((16, LANES), both, I32) == 1, out[at], middle[k])
 
 
 def gain_of(q):
@@ -558,11 +564,14 @@
                 return f_in[x, (sy - 3) * e]
 
             for X in range(cx):
-                s_buf[QPAD * X : QPAD * X + Q] = ((f_buf[2 * X, e] + f_buf[2 * X + 1, e])
-                                                  + (beside(2 * X) + beside(2 * X + 1)))
-            mean = dot_exact(s_buf[...], thin[...])
+                at = QPAD * (cx * e + X)
+                s_buf[at : at + Q] = ((f_buf[2 * X, e] + f_buf[2 * X + 1, e])
+                                      + (beside(2 * X) + beside(2 * X + 1)))
+        mean = dot_parts(s_buf[...], thin[...], 2)
+        for e in range(2):
             for X in range(cx):
-                c_buf[X, e] = mean[QPAD * X : QPAD * X + Q, 0:nzc]
+                at = QPAD * (cx * e + X)
+                c_buf[X, e] = mean[at : at + Q, 0:nzc]
             coarse_copy(e).start()
         for c in ready + fixed[0] + fixed[1]:
             c.wait()
@@ -596,8 +605,36 @@
                 return c_g[q, 1]
             return c_all[q, J - 1]
 
+        lower = sub < 4
+
+        def joined(a, b, by):
+            return jnp.where(lower, roll_sub(a, by), roll_sub(b, by + 4))
+
+        lane = iota(1)
+        edges = {1: lane == 0, -1: lane == nzc - 1}
+        none = jnp.zeros((8, LANES), I32)
+        center = [joined(plane(q, 1), plane(q, cy), 0) for q in range(Q)]
+        pulled = []
+        for q in range(Q):
+            ex, ey, ez = STEP[q]
+            if (ex, ey, ez) == (0, 0, 0):
+                pulled.append(center[q])
+                continue
+            v = roll_lane(joined(plane(q, 1 - ey), plane(q, cy - ey), ex), ez)
+            m = None
+            if ey != 0:
+                walls = (wall, none) if ey < 0 else (none, wall)
+                m = roll_lane(joined(*walls, ex), ez) == 1
+            if ez != 0:
+                m = edges[ez] if m is None else m | edges[ez]
+            pulled.append(v if m is None else jnp.where(m, center[26 - q], v))
+        new = collide(pulled, coef)
+        for q0, n in OCTETS:
+            tile = jnp.swapaxes(jnp.stack(new[q0 : q0 + n]), 0, 1)
+            for e in range(2):
+                for X in range(cx):
+                    c_buf[X, e, q0 : q0 + n] = tile[1 + X + 4 * e][:, 0:nzc]
         for e in range(2):
-            coarse_step(plane, 1 if e == 0 else cy, wall, coef, c_buf, e, nzc, cx, 2)
             coarse_copy(e).start()
 
     for e in range(2):
@@ -626,10 +663,11 @@
         in_specs=[ANY] * 3,
         out_specs=(VMEM, VMEM),
         scratch_shapes=[
-            pltpu.VMEM((sy, Q, nz), F32),
-            pltpu.VMEM((sy, Q, nz), F32),
+            pltpu.VMEM((sy, 16, nz), F32),
+            pltpu.VMEM((sy, Q - 16, nz), F32),
             pltpu.VMEM((cy, Q, nzc), F32),
             pltpu.VMEM((cy, Q, nzc), F32),
+            pltpu.VMEM((2, 16, LANES), F32),
             pltpu.SMEM(block_level.shape, I32),
             pltpu.SemaphoreType.DMA((5,)),
         ],
@@ -713,7 +751,7 @@
             pltpu.VMEM((Q, 2, 8, LANES), F32),
             pltpu.VMEM((sx, 2, Q, nz), F32),
             pltpu.VMEM((2, 2, Q, nz), F32),
-            pltpu.VMEM((QPAD * cx, nz), F32),
+            pltpu.VMEM((2 * QPAD * cx, nz), F32),
             pltpu.VMEM((cx, 2, Q, nzc), F32),
             pltpu.SemaphoreType.DMA((10,)),
         ],

time: 16 us -> 15.8 us (0.988)
  Pallas kernels: 4.77 us -> 4.58 us
where the time goes in v5:
time: 15.8 us; the launch traced here: 15.6 us
  starting transfers between devices  5.95 us (38%)
  Pallas kernels  4.58 us (29%)
  waiting for transfers between devices  3.67 us (23%)
  local copies, waits for them, and re-layouts  0.75 us (5%)
  between operations  0.69 us (4%)
    ppermute x1, starting transfers between devices, local(): from_low = lax.ppermute(up, 'stream', ring('stream', 1))  3.02 us
    ppermute x1, waiting for transfers between devices, local(): second = lax.ppermute(second, 'span', pairs('span', 1))  2.27 us
    ppermute x1, starting transfers between devices, local(): second = lax.ppermute(second, 'span', pairs('span', 1))  1.9 us
    pallas_call x1, Pallas kernels, local(): pl.pallas_call(outer_kernel, out_shape=(fine_shape, coarse_shape), in_spe...  1.31 us
    pallas_call x1, Pallas kernels, local(): pl.pallas_call(inner_kernel, out_shape=(fine_shape, coarse_shape, struct(...  1.18 us
    pallas_call x1, Pallas kernels, local(): pl.pallas_call(pack_x_kernel, out_shape=(x_message, x_message), in_specs=...  1.09 us
    ppermute x1, waiting for transfers between devices, local(): from_high = lax.ppermute(down, 'stream', ring('stream', -1))  1.06 us
    ppermute x1, starting transfers between devices, local(): from_high = lax.ppermute(down, 'stream', ring('stream', -1))  1.02 us
  transfers between devices with their start and end apart: 4, of which 3 were waited for; matrix products, arithmetic and copies ran while one was open for 0% of the time, Pallas kernels for 13%

profile of v5, /device:TPU:0, one launch (start us, length us, event | category | flops | bytes accessed | tf_op | source)
XLA Modules:
  0.0 15.6 jit_solution(12324674311340810523)
XLA Ops:
  0.6 0.0 copy-start
  0.6 0.0 copy-start.1
  0.6 1.1 %pack_x.1 = (f32[88,128]{1,0:T(8,128)S(1)}, f32[88,128]{1,0:T(8,128)S(1)}) custom-call(f32[6,6,27,128]{3,2,1,0:T(8,128)} %bitcast.4, f32[3,3,27,64]{3,2,1,0:T(8,128)} %bitcast.7, s32[4,8]{1,0:T(4,128)} %level.3), custom_call_target="tpu_custom_call" | custom-call | tf_op jit(solution)/shard_map/pack_x/pallas_call | solution.py:660
  1.7 0.0 copy-start.3
  1.8 0.0 copy-start.4
  1.8 3.0 %collective-permute-start = (f32[88,128]{1,0:T(8,128)S(1)}, f32[88,128]{1,0:T(8,128)S(1)}, u32[]{:S(2)}, u32[]{:S(2)}) collective-permute-start(f32[88,128]{1,0:T(8,128)S(1)} %get-tuple-element.23), channel_id=1, source_target_pairs={{0,8},{8,16},{16,24},{24,0},{1,9},{9,17},{17,25},{25,1},{2,10},{10... | collective-permute-start | bytes 135176 | tf_op jit(solution)/shard_map/ppermute | solution.py:677
  4.8 1.0 %collective-permute-start.1 = (f32[88,128]{1,0:T(8,128)S(1)}, f32[88,128]{1,0:T(8,128)S(1)}, u32[]{:S(2)}, u32[]{:S(2)}) collective-permute-start(f32[88,128]{1,0:T(8,128)S(1)} %get-tuple-element.24), channel_id=1, source_target_pairs={{0,24},{8,0},{16,8},{24,16},{1,25},{9,1},{17,9},{25,17},{2,26},{10... | collective-permute-start | bytes 135176 | tf_op jit(solution)/shard_map/ppermute | solution.py:678
  5.8 0.0 copy-done.1
  5.8 0.0 copy-done.3
  5.8 0.0 copy-done.4
  5.8 0.0 copy-start.2
  5.8 0.7 %copy-done.2 = s32[6,6,128]{2,1,0:T(8,128)S(1)} copy-done((s32[6,6,128]{2,1,0:T(8,128)S(1)}, s32[6,6,128]{2,1,0:T(8,128)}, u32[]{:S(2)}) %copy-start.2) | copy-done | bytes 18456
  6.6 0.9 %tables.1 = (s32[9,8,128]{2,1,0:T(8,128)S(1)}, f32[35,8,128]{2,1,0:T(8,128)S(1)}, s32[2,8,128]{2,1,0:T(8,128)S(1)}, s32[8,128]{1,0:T(8,128)S(1)}, f32[3,3,32,128...) custom-call(f32[3,3,27,64]{3,2,1,0:T(8,128)S(1)} %bitcast.8, ...), custom_call_target="tpu_custom_call" | custom-call | flops 10000000 | bytes 1000000 | tf_op jit(solution)/shard_map/tables/pallas_call | solution.py:680
  7.4 0.3 %collective-permute-done.from_low = f32[88,128]{1,0:T(8,128)S(1)} collective-permute-done((f32[88,128]{1,0:T(8,128)S(1)}, f32[88,128]{1,0:T(8,128)S(1)}, u32[]{:S(2)}, u32[]{:S(2)}) %collective-permute-start) | collective-permute-done | bytes 45088 | tf_op jit(solution)/shard_map/ppermute | solution.py:677
  7.8 1.1 %collective-permute-done.1.from_high = f32[88,128]{1,0:T(8,128)S(1)} collective-permute-done((f32[88,128]{1,0:T(8,128)S(1)}, f32[88,128]{1,0:T(8,128)S(1)}, u32[]{:S(2)}, u32[]{:S(2)}) %collective-permute-start.1) | collective-permute-done | bytes 45088 | tf_op jit(solution)/shard_map/ppermute | solution.py:678
  8.8 0.0 copy-done
  8.8 0.1 pack_y.1
  8.9 1.9 %collective-permute-start.2 = (f32[80,128]{1,0:T(8,128)S(1)}, f32[80,128]{1,0:T(8,128)S(1)}, u32[]{:S(2)}, u32[]{:S(2)}) collective-permute-start(f32[80,128]{1,0:T(8,128)S(1)} %get-tuple-element.26), channel_id=1, source_target_pairs={{0,7},{1,2},{2,1},{3,4},{4,3},{5,6},{6,5},{7,0},{8,15},{9,10},{10,... | collective-permute-start | bytes 122888 | tf_op jit(solution)/shard_map/ppermute | solution.py:709
  10.9 0.0 collective-permute-start.3
  10.9 1.2 %inner.1 = (f32[6,6,27,128]{3,2,1,0:T(8,128)}, f32[3,3,27,64]{3,2,1,0:T(8,128)}, f32[27,4,8,128]{3,2,1,0:T(8,128)S(1)}, f32[2,8,32,128]{3,2,1,0:T(8,128)S(1)}, f...) custom-call(f32[6,6,27,128]{3,2,1,0:T(8,128)S(1)} %bitcast.6, ...), custom_call_target="tpu_custom_call" | custom-call | flops 20000000 | bytes 1000000 | tf_op jit(solution)/shard_map/inner/pallas_call | solution.py:716
  12.0 2.3 %collective-permute-done.2.second = f32[80,128]{1,0:T(8,128)S(1)} collective-permute-done((f32[80,128]{1,0:T(8,128)S(1)}, f32[80,128]{1,0:T(8,128)S(1)}, u32[]{:S(2)}, u32[]{:S(2)}) %collective-permute-start.2) | collective-permute-done | bytes 40992 | tf_op jit(solution)/shard_map/ppermute | solution.py:709
  14.3 0.0 collective-permute-done.3.first
  14.3 1.3 %outer.1 = (f32[6,6,27,128]{3,2,1,0:T(8,128)}, f32[3,3,27,64]{3,2,1,0:T(8,128)}) custom-call(f32[80,128]{1,0:T(8,128)S(1)} %collective-permute-done.2.second, f32[80,128]{1,0:T(8,128)S(1)} %collective-permute-done.3.first, f32[27,2,8,128]{3,2,1,0:T(8,128)S(1)} %get-tuple-element.28.w_edge, ...), custom_call_target="tpu_custom_call", output_to_operand_aliasing={{0}: (13, {}), {1}: (14, {})} | custom-call | tf_op jit(solution)/shard_map/outer/pallas_call | solution.py:740
Async XLA Ops:
  0.6 8.2 %copy-start = (f32[27,6,6,128]{3,0,2,1:T(8,128)S(1)}, f32[27,6,6,128]{3,0,2,1:T(8,128)}, u32[]{:S(2)}) copy-start(f32[27,6,6,128]{3,0,2,1:T(8,128)} %param.5) | copy-start | bytes 1492996
  0.6 5.2 %copy-start.1 = (f32[27,3,3,64]{3,0,2,1:T(8,128)S(1)}, f32[27,3,3,64]{3,0,2,1:T(8,128)}, u32[]{:S(2)}) copy-start(f32[27,3,3,64]{3,0,2,1:T(8,128)} %param.6) | copy-start | bytes 186628
  1.7 4.1 %copy-start.3 = (s32[4,8]{1,0:T(4,128)S(1)}, s32[4,8]{1,0:T(4,128)}, u32[]{:S(2)}) copy-start(s32[4,8]{1,0:T(4,128)} %level.3) | copy-start | bytes 388
  1.8 4.1 %copy-start.4 = (f32[27]{0:T(128)S(1)}, f32[27]{0:T(128)}, u32[]{:S(2)}) copy-start(f32[27]{0:T(128)} %rates.1) | copy-start | bytes 328
  1.8 6.0 %collective-permute-start = (f32[88,128]{1,0:T(8,128)S(1)}, f32[88,128]{1,0:T(8,128)S(1)}, u32[]{:S(2)}, u32[]{:S(2)}) collective-permute-start(f32[88,128]{1,0:T(8,128)S(1)} %get-tuple-element.23), channel_id=1, source_target_pairs={{0,8},{8,16},{16,24},{24,0},{1,9},{9,17},{17,25},{25,1},{2,10},{10... | collective-permute-start | bytes 135176 | tf_op jit(solution)/shard_map/ppermute | solution.py:677
  4.8 4.0 %collective-permute-start.1 = (f32[88,128]{1,0:T(8,128)S(1)}, f32[88,128]{1,0:T(8,128)S(1)}, u32[]{:S(2)}, u32[]{:S(2)}) collective-permute-start(f32[88,128]{1,0:T(8,128)S(1)} %get-tuple-element.24), channel_id=1, source_target_pairs={{0,24},{8,0},{16,8},{24,16},{1,25},{9,1},{17,9},{25,17},{2,26},{10... | collective-permute-start | bytes 135176 | tf_op jit(solution)/shard_map/ppermute | solution.py:678
  5.8 0.7 %copy-start.2 = (s32[6,6,128]{2,1,0:T(8,128)S(1)}, s32[6,6,128]{2,1,0:T(8,128)}, u32[]{:S(2)}) copy-start(s32[6,6,128]{2,1,0:T(8,128)} %obstacle.1) | copy-start | bytes 55300
  8.9 5.4 %collective-permute-start.2 = (f32[80,128]{1,0:T(8,128)S(1)}, f32[80,128]{1,0:T(8,128)S(1)}, u32[]{:S(2)}, u32[]{:S(2)}) collective-permute-start(f32[80,128]{1,0:T(8,128)S(1)} %get-tuple-element.26), channel_id=1, source_target_pairs={{0,7},{1,2},{2,1},{3,4},{4,3},{5,6},{6,5},{7,0},{8,15},{9,10},{10,... | collective-permute-start | bytes 122888 | tf_op jit(solution)/shard_map/ppermute | solution.py:709
  10.9 3.5 %collective-permute-start.3 = (f32[80,128]{1,0:T(8,128)S(1)}, f32[80,128]{1,0:T(8,128)S(1)}, u32[]{:S(2)}, u32[]{:S(2)}) collective-permute-start(f32[80,128]{1,0:T(8,128)S(1)} %get-tuple-element.27), channel_id=1, source_target_pairs={{0,1},{1,0},{2,3},{3,2},{4,5},{5,4},{6,7},{7,6},{8,9},{9,8},{10,11... | collective-permute-start | bytes 122888 | tf_op jit(solution)/shard_map/ppermute | solution.py:710

commit v6 on v5

--- a/solution.py
+++ b/solution.py
@@ -130,7 +130,12 @@
         1.0 if q % 3 == 0 else 1.0 / 3.0)
 
 
-def tables_kernel(coarse, obstacle, level, rates, levels, coef, flags, c_wall, c_wide, refine, thin):
+def tables_kernel(fine_far, coarse_far, obstacle_far, level, rates,
+                  levels, coef, flags, c_wall, c_wide, refine, thin, fine, coarse, obstacle, sems):
+    arrive = [pltpu.make_async_copy(a, b, sems.at[k]) for k, (a, b) in enumerate(
+        ((obstacle_far, obstacle), (coarse_far, coarse), (fine_far, fine)))]
+    for c in arrive:
+        c.start()
     cx, cy, nzc = coarse.shape[0], coarse.shape[1], coarse.shape[3]
     sx, sy, nz = obstacle.shape
     row, col = lax.axis_index("stream"), lax.axis_index("span")
@@ -153,6 +158,15 @@
         coef[q] = 0.125 - 0.125 * s
         if q in EVEN:
             coef[Q + EVEN.index(q)] = (0.125 * gain_of(q)) * s
+    shape = (2 * nzc, 2 * nz)
+    i, l = iota(0, shape), iota(1, shape)
+    half, l = l // nz, l % nz
+    za = (l >> 1) + half * nzc
+    zb = jnp.clip((l >> 1) + jnp.where((l & 1) == 1, 1, -1), 0, nzc - 1) + half * nzc
+    refine[...] = (jnp.where(i == za, 0.75, 0.0) + jnp.where(i == zb, 0.25, 0.0)).astype(BF16)
+    shape = (nz, nz)
+    thin[...] = jnp.where((iota(0, shape) >> 1) == iota(1, shape), 0.125, 0.0).astype(BF16)
+    arrive[0].wait()
     planes = []
     for k, y in enumerate((sy // 2 - 1, sy // 2)):
         v = jnp.zeros((8, LANES), I32)
@@ -166,17 +180,11 @@
     both = jnp.take_along_axis(both, (2 * lane) & (LANES - 1), axis=1)
     both = jnp.broadcast_to(both[sx // 2 : sx // 2 + 1], (8, LANES))
     c_wall[...] = jnp.where((sub == 1 + cx // 2) & (lane < nzc), both, 0)
-    shape = (2 * nzc, 2 * nz)
-    i, l = iota(0, shape), iota(1, shape)
-    half, l = l // nz, l % nz
-    za = (l >> 1) + half * nzc
-    zb = jnp.clip((l >> 1) + jnp.where((l & 1) == 1, 1, -1), 0, nzc - 1) + half * nzc
-    refine[...] = (jnp.where(i == za, 0.75, 0.0) + jnp.where(i == zb, 0.25, 0.0)).astype(BF16)
-    shape = (nz, nz)
-    thin[...] = jnp.where((iota(0, shape) >> 1) == iota(1, shape), 0.125, 0.0).astype(BF16)
+    arrive[1].wait()
     for Y in range(cy):
         for X in range(cx):
             c_wide[Y, X, 0:Q] = dot_exact(coarse[X, Y], refine[0:nzc, 0:nz])
+    arrive[2].wait()
 
 
 def fine_plane(fine, from_low, from_high, y, mixed=None):
@@ -677,7 +685,8 @@
     from_low = lax.ppermute(up, "stream", ring("stream", 1))
     from_high = lax.ppermute(down, "stream", ring("stream", -1))
 
-    levels, coef, flags, c_wall, c_wide, refine, thin = pl.pallas_call(
+    fine_shape, coarse_shape = struct(fine.shape), struct(coarse.shape)
+    levels, coef, flags, c_wall, c_wide, refine, thin, fine, coarse = pl.pallas_call(
         tables_kernel,
         out_shape=(
             struct((9, 8, LANES), I32),
@@ -687,13 +696,16 @@
             struct((cy, cx, QPAD, nz)),
             struct((2 * nzc, 2 * nz), BF16),
             struct((nz, nz), BF16),
+            fine_shape,
+            coarse_shape,
         ),
-        in_specs=[VMEM] * 2 + [SMEM] * 2,
-        out_specs=(VMEM,) * 7,
+        in_specs=[ANY] * 3 + [SMEM] * 2,
+        out_specs=(VMEM,) * 9,
+        scratch_shapes=[pltpu.VMEM(obstacle.shape, I32), pltpu.SemaphoreType.DMA((3,))],
         compiler_params=params(),
         cost_estimate=cost(10_000_000, 1_000_000),
         name="tables",
-    )(coarse, obstacle, block_level, relax_rates)
+    )(in_hbm(fine), in_hbm(coarse), in_hbm(obstacle), block_level, relax_rates)
 
     y_message = struct((Y_ROWS, LANES))
     second, first, w_edge = pl.pallas_call(
@@ -712,7 +724,6 @@
         second, first = (lax.ppermute(first, "span", ring("span", 1)),
                          lax.ppermute(second, "span", ring("span", -1)))
 
-    fine_shape, coarse_shape = struct(fine.shape), struct(coarse.shape)
     out, c_out, w_in, ex_side, c_all, f_in, aux = pl.pallas_call(
         inner_kernel,
         out_shape=(

time: 15.8 us -> 15.8 us (level)
  Pallas kernels: 4.58 us -> 5.36 us
  local copies, waits for them, and re-layouts: 0.75 us -> 0.01 us
    pallas_call x1, Pallas kernels: 0.88 us -> 1.76 us  [local(): pl.pallas_call(tables_kernel, out_shape=(struct((9, 8, LANES), I32), stru...]
    unnamed x10 -> x4, local copies, waits for them, and re-layouts: 0.75 us -> 0.01 us
  transfers between devices with their start and end apart: 4 -> 4, of which waited for: 3 -> 3; matrix products, arithmetic and copies ran while one was open for 0% -> 0% of each run, Pallas kernels for 13% -> 19%
where the time goes in v6:
time: 15.8 us; the launch traced here: 15.5 us
  starting transfers between devices  5.95 us (38%)
  Pallas kernels  5.36 us (34%)
  waiting for transfers between devices  3.53 us (22%)
  between operations  0.68 us (4%)
    ppermute x1, starting transfers between devices, local(): from_low = lax.ppermute(up, 'stream', ring('stream', 1))  3.02 us
    ppermute x1, waiting for transfers between devices, local(): second = lax.ppermute(second, 'span', pairs('span', 1))  2.27 us
    ppermute x1, starting transfers between devices, local(): second = lax.ppermute(second, 'span', pairs('span', 1))  1.9 us
    pallas_call x1, Pallas kernels, local(): pl.pallas_call(tables_kernel, out_shape=(struct((9, 8, LANES), I32), stru...  1.76 us
    pallas_call x1, Pallas kernels, local(): pl.pallas_call(outer_kernel, out_shape=(fine_shape, coarse_shape), in_spe...  1.31 us
    pallas_call x1, Pallas kernels, local(): pl.pallas_call(inner_kernel, out_shape=(fine_shape, coarse_shape, struct(...  1.18 us
    ppermute x1, waiting for transfers between devices, local(): from_high = lax.ppermute(down, 'stream', ring('stream', -1))  1.06 us
    ppermute x1, starting transfers between devices, local(): from_high = lax.ppermute(down, 'stream', ring('stream', -1))  1.02 us
  transfers between devices with their start and end apart: 4, of which 3 were waited for; matrix products, arithmetic and copies ran while one was open for 0% of the time, Pallas kernels for 19%

profile of v6, /device:TPU:0, one launch (start us, length us, event | category | flops | bytes accessed | tf_op | source)
XLA Modules:
  0.0 15.5 jit_solution(13905837755056662736)
XLA Ops:
  0.6 1.0 %pack_x.1 = (f32[88,128]{1,0:T(8,128)S(1)}, f32[88,128]{1,0:T(8,128)S(1)}) custom-call(f32[6,6,27,128]{3,2,1,0:T(8,128)} %bitcast.4, f32[3,3,27,64]{3,2,1,0:T(8,128)} %bitcast.7, s32[4,8]{1,0:T(4,128)} %level.3), custom_call_target="tpu_custom_call" | custom-call | tf_op jit(solution)/shard_map/pack_x/pallas_call | solution.py:668
  1.6 0.0 copy-start
  1.7 0.0 copy-start.1
  1.7 3.0 %collective-permute-start = (f32[88,128]{1,0:T(8,128)S(1)}, f32[88,128]{1,0:T(8,128)S(1)}, u32[]{:S(2)}, u32[]{:S(2)}) collective-permute-start(f32[88,128]{1,0:T(8,128)S(1)} %get-tuple-element.27), channel_id=1, source_target_pairs={{0,8},{8,16},{16,24},{24,0},{1,9},{9,17},{17,25},{25,1},{2,10},{10... | collective-permute-start | bytes 135176 | tf_op jit(solution)/shard_map/ppermute | solution.py:685
  4.7 1.0 %collective-permute-start.1 = (f32[88,128]{1,0:T(8,128)S(1)}, f32[88,128]{1,0:T(8,128)S(1)}, u32[]{:S(2)}, u32[]{:S(2)}) collective-permute-start(f32[88,128]{1,0:T(8,128)S(1)} %get-tuple-element.28), channel_id=1, source_target_pairs={{0,24},{8,0},{16,8},{24,16},{1,25},{9,1},{17,9},{25,17},{2,26},{10... | collective-permute-start | bytes 135176 | tf_op jit(solution)/shard_map/ppermute | solution.py:686
  5.7 0.0 copy-done
  5.7 0.0 copy-done.1
  5.7 1.8 %tables.1 = (s32[9,8,128]{2,1,0:T(8,128)S(1)}, f32[35,8,128]{2,1,0:T(8,128)S(1)}, s32[2,8,128]{2,1,0:T(8,128)S(1)}, s32[8,128]{1,0:T(8,128)S(1)}, f32[3,3,32,128...) custom-call(f32[6,6,27,128]{3,2,1,0:T(8,128)} %bitcast.5, ...), custom_call_target="tpu_custom_call" | custom-call | flops 10000000 | bytes 1000000 | tf_op jit(solution)/shard_map/tables/pallas_call | solution.py:689
  7.5 0.2 %collective-permute-done.from_low = f32[88,128]{1,0:T(8,128)S(1)} collective-permute-done((f32[88,128]{1,0:T(8,128)S(1)}, f32[88,128]{1,0:T(8,128)S(1)}, u32[]{:S(2)}, u32[]{:S(2)}) %collective-permute-start) | collective-permute-done | bytes 45088 | tf_op jit(solution)/shard_map/ppermute | solution.py:685
  7.7 1.1 %collective-permute-done.1.from_high = f32[88,128]{1,0:T(8,128)S(1)} collective-permute-done((f32[88,128]{1,0:T(8,128)S(1)}, f32[88,128]{1,0:T(8,128)S(1)}, u32[]{:S(2)}, u32[]{:S(2)}) %collective-permute-start.1) | collective-permute-done | bytes 45088 | tf_op jit(solution)/shard_map/ppermute | solution.py:686
  8.7 0.1 pack_y.1
  8.8 1.9 %collective-permute-start.2 = (f32[80,128]{1,0:T(8,128)S(1)}, f32[80,128]{1,0:T(8,128)S(1)}, u32[]{:S(2)}, u32[]{:S(2)}) collective-permute-start(f32[80,128]{1,0:T(8,128)S(1)} %get-tuple-element.30), channel_id=1, source_target_pairs={{0,7},{1,2},{2,1},{3,4},{4,3},{5,6},{6,5},{7,0},{8,15},{9,10},{10,... | collective-permute-start | bytes 122888 | tf_op jit(solution)/shard_map/ppermute | solution.py:721
  10.7 0.0 collective-permute-start.3
  10.8 1.2 %inner.1 = (f32[6,6,27,128]{3,2,1,0:T(8,128)}, f32[3,3,27,64]{3,2,1,0:T(8,128)}, f32[27,4,8,128]{3,2,1,0:T(8,128)S(1)}, f32[2,8,32,128]{3,2,1,0:T(8,128)S(1)}, f...) custom-call(f32[6,6,27,128]{3,2,1,0:T(8,128)S(1)} %get-tuple-element.25.fine, ...), custom_call_target="tpu_custom_call" | custom-call | flops 20000000 | bytes 1000000 | tf_op jit(solution)/shard_map/inner/pallas_call | solution.py:727
  11.9 2.3 %collective-permute-done.2.second = f32[80,128]{1,0:T(8,128)S(1)} collective-permute-done((f32[80,128]{1,0:T(8,128)S(1)}, f32[80,128]{1,0:T(8,128)S(1)}, u32[]{:S(2)}, u32[]{:S(2)}) %collective-permute-start.2) | collective-permute-done | bytes 40992 | tf_op jit(solution)/shard_map/ppermute | solution.py:721
  14.2 0.0 collective-permute-done.3.first
  14.2 1.3 %outer.1 = (f32[6,6,27,128]{3,2,1,0:T(8,128)}, f32[3,3,27,64]{3,2,1,0:T(8,128)}) custom-call(f32[80,128]{1,0:T(8,128)S(1)} %collective-permute-done.2.second, f32[80,128]{1,0:T(8,128)S(1)} %collective-permute-done.3.first, f32[27,2,8,128]{3,2,1,0:T(8,128)S(1)} %get-tuple-element.32.w_edge, ...), custom_call_target="tpu_custom_call", output_to_operand_aliasing={{0}: (13, {}), {1}: (14, {})} | custom-call | tf_op jit(solution)/shard_map/outer/pallas_call | solution.py:751
Async XLA Ops:
  1.6 4.1 %copy-start = (s32[4,8]{1,0:T(4,128)S(1)}, s32[4,8]{1,0:T(4,128)}, u32[]{:S(2)}) copy-start(s32[4,8]{1,0:T(4,128)} %level.3) | copy-start | bytes 388
  1.7 4.1 %copy-start.1 = (f32[27]{0:T(128)S(1)}, f32[27]{0:T(128)}, u32[]{:S(2)}) copy-start(f32[27]{0:T(128)} %rates.1) | copy-start | bytes 328
  1.7 6.0 %collective-permute-start = (f32[88,128]{1,0:T(8,128)S(1)}, f32[88,128]{1,0:T(8,128)S(1)}, u32[]{:S(2)}, u32[]{:S(2)}) collective-permute-start(f32[88,128]{1,0:T(8,128)S(1)} %get-tuple-element.27), channel_id=1, source_target_pairs={{0,8},{8,16},{16,24},{24,0},{1,9},{9,17},{17,25},{25,1},{2,10},{10... | collective-permute-start | bytes 135176 | tf_op jit(solution)/shard_map/ppermute | solution.py:685
  4.7 4.0 %collective-permute-start.1 = (f32[88,128]{1,0:T(8,128)S(1)}, f32[88,128]{1,0:T(8,128)S(1)}, u32[]{:S(2)}, u32[]{:S(2)}) collective-permute-start(f32[88,128]{1,0:T(8,128)S(1)} %get-tuple-element.28), channel_id=1, source_target_pairs={{0,24},{8,0},{16,8},{24,16},{1,25},{9,1},{17,9},{25,17},{2,26},{10... | collective-permute-start | bytes 135176 | tf_op jit(solution)/shard_map/ppermute | solution.py:686
  8.8 5.4 %collective-permute-start.2 = (f32[80,128]{1,0:T(8,128)S(1)}, f32[80,128]{1,0:T(8,128)S(1)}, u32[]{:S(2)}, u32[]{:S(2)}) collective-permute-start(f32[80,128]{1,0:T(8,128)S(1)} %get-tuple-element.30), channel_id=1, source_target_pairs={{0,7},{1,2},{2,1},{3,4},{4,3},{5,6},{6,5},{7,0},{8,15},{9,10},{10,... | collective-permute-start | bytes 122888 | tf_op jit(solution)/shard_map/ppermute | solution.py:721
  10.7 3.5 %collective-permute-start.3 = (f32[80,128]{1,0:T(8,128)S(1)}, f32[80,128]{1,0:T(8,128)S(1)}, u32[]{:S(2)}, u32[]{:S(2)}) collective-permute-start(f32[80,128]{1,0:T(8,128)S(1)} %get-tuple-element.31), channel_id=1, source_target_pairs={{0,1},{1,0},{2,3},{3,2},{4,5},{5,4},{6,7},{7,6},{8,9},{9,8},{10,11... | collective-permute-start | bytes 122888 | tf_op jit(solution)/shard_map/ppermute | solution.py:722

commit v7 on v6

--- a/solution.py
+++ b/solution.py
@@ -28,6 +28,7 @@
 LEV_X_LOW, LEV_X_HIGH, LEV_OWN, LEV_Y_LOW, LEV_Y_HIGH, EVEN_SPAN = 3, 4, 5, 6, 7, 8
 
 X_FINE, X_MIDDLE = Q, Q + 9
+SPARE = (3, 24)
 Y_SECOND, Y_THIRD, Y_CORNER = Q, 2 * Q, 2 * Q + 16
 Y_ROWS = 80
 
@@ -110,19 +111,27 @@
         c.wait()
     cy, nzc = c_low.shape[0], c_low.shape[2]
     for k, (out, f, c, q0) in enumerate(((up, f_high, c_high, HIGH_X[0] - 16), (down, f_low, c_low, LOW_X[0]))):
-        middle[k, :, 0:nzc] = c[1, 0:16]
+        middle[k, 0:16, 0:nzc] = c[1, 0:16]
         middle[k, 0 : Q - 16, nzc : 2 * nzc] = c[1, 16:Q]
         out[0:Q, 0:nzc] = c[0]
         out[0:Q, nzc : 2 * nzc] = c[cy - 1]
+        middle[k, 16:17] = f[sy - 1, q0 + 8 : q0 + 9]
         for y in range(sy):
-            out[X_FINE + 9 * y : X_FINE + 9 * y + 9] = f[y, q0 : q0 + 9]
+            n = 9 if y < sy - 1 else 8
+            out[X_FINE + 9 * y : X_FINE + 9 * y + n] = f[y, q0 : q0 + n]
     fetch_level.wait()
-    n_row = lev.shape[0]
+    n_row, n_col = lev.shape
     row, col = lax.axis_index("stream"), lax.axis_index("span")
+    high_half = iota(1, (2, LANES)) >= nzc
     for k, (out, to) in enumerate(((up, row + 1), (down, row + n_row - 1))):
         both = lev[row, col] * lev[lax.rem(to, n_row), col]
-        at = slice(X_MIDDLE, X_MIDDLE + 16)
-        out[at] = jnp.where(jnp.full((16, LANES), both, I32) == 1, out[at], middle[k])
+        on = both * lev[lax.rem(to, n_row), lax.rem(col + 1, n_col)]
+        at = slice(X_MIDDLE, X_MIDDLE + 17)
+        out[at] = jnp.where(jnp.full((17, LANES), both, I32) == 1, out[at], middle[k])
+        last = middle[k, 16:17]
+        at = slice(SPARE[k], SPARE[k] + 2)
+        spare = jnp.concatenate([roll_lane(last, nzc), last], axis=0)
+        out[at] = jnp.where(high_half & (jnp.full((2, LANES), on, I32) == 1), spare, out[at])
 
 
 def gain_of(q):
@@ -187,7 +196,7 @@
     arrive[2].wait()
 
 
-def fine_plane(fine, from_low, from_high, y, mixed=None):
+def fine_plane(fine, from_low, from_high, y, mixed=None, last=None):
     sx = fine.shape[0]
     base = X_FINE + 9 * y
     rows = [None] * Q
@@ -197,11 +206,11 @@
         if q0 == 16:
             low = from_low[base - 2 : base + 6]
         if q0 == 24:
-            low = from_low[base + 6 : base + 9]
+            low = from_low[base + 6 : base + 9] if last is None else jnp.concatenate([from_low[base + 6 : base + 8], last[0]], axis=0)
         if q0 == 0:
             high = from_high[base : base + 8]
         if q0 == 8:
-            high = row8(from_high, base + 8)
+            high = row8(from_high, base + 8) if last is None else jnp.broadcast_to(last[1], (8, LANES))
         if mixed is not None:
             if q0 >= 16:
                 low = mixed(0, q0, n, low)
@@ -240,7 +249,15 @@
         out[Y_SECOND : Y_SECOND + Q, 0:nzc] = coarse[2, Y]
         out[Y_THIRD : Y_THIRD + 16, 0:nzc] = coarse[1, Y, 0:16]
         out[Y_THIRD : Y_THIRD + Q - 16, nzc : 2 * nzc] = coarse[1, Y, 16:Q]
-        rows = fine_plane(fine, from_low, from_high, y)
+        last = None
+        if e == 1:
+            last = []
+            for side, msg, near in ((0, from_low, LEV_X_LOW), (1, from_high, LEV_X_HIGH)):
+                at = SPARE[side]
+                halves = jnp.where(low_half[0:1], roll_lane(msg[at : at + 1], nzc), msg[at + 1 : at + 2])
+                packed = (levels[LEV_OWN] * levels[near])[0:1] == 1
+                last.append(jnp.where(packed, halves, msg[X_MIDDLE + 16 : X_MIDDLE + 17]))
+        rows = fine_plane(fine, from_low, from_high, y, last=last)
         for q in range(Q):
             w_edge[q, e] = rows[q]
         for k in range(3):
@@ -664,7 +681,7 @@
     sx, sy, _, nz = fine.shape
     cx, cy, _, nzc = coarse.shape
 
-    x_message = struct((8 * ((X_FINE + 9 * sy + 7) // 8), LANES))
+    x_message = struct((X_FINE + 9 * sy - 1, LANES))
     up, down = pl.pallas_call(
         pack_x_kernel,
         out_shape=(x_message, x_message),
@@ -675,7 +692,7 @@
             pltpu.VMEM((sy, Q - 16, nz), F32),
             pltpu.VMEM((cy, Q, nzc), F32),
             pltpu.VMEM((cy, Q, nzc), F32),
-            pltpu.VMEM((2, 16, LANES), F32),
+            pltpu.VMEM((2, 17, LANES), F32),
             pltpu.SMEM(block_level.shape, I32),
             pltpu.SemaphoreType.DMA((5,)),
         ],

time: 15.8 us -> 15.7 us (level)
  no operation moved by 1% of the time
where the time goes in v7:
time: 15.7 us; the launch traced here: 15.5 us
  starting transfers between devices  5.9 us (38%)
  Pallas kernels  5.41 us (34%)
  waiting for transfers between devices  3.53 us (22%)
  between operations  0.67 us (4%)
    ppermute x1, starting transfers between devices, local(): from_low = lax.ppermute(up, 'stream', ring('stream', 1))  3.02 us
    ppermute x1, waiting for transfers between devices, local(): second = lax.ppermute(second, 'span', pairs('span', 1))  2.32 us
    ppermute x1, starting transfers between devices, local(): second = lax.ppermute(second, 'span', pairs('span', 1))  1.86 us
    pallas_call x1, Pallas kernels, local(): pl.pallas_call(tables_kernel, out_shape=(struct((9, 8, LANES), I32), stru...  1.76 us
    pallas_call x1, Pallas kernels, local(): pl.pallas_call(outer_kernel, out_shape=(fine_shape, coarse_shape), in_spe...  1.31 us
    pallas_call x1, Pallas kernels, local(): pl.pallas_call(inner_kernel, out_shape=(fine_shape, coarse_shape, struct(...  1.18 us
    ppermute x1, waiting for transfers between devices, local(): from_high = lax.ppermute(down, 'stream', ring('stream', -1))  1.06 us
    pallas_call x1, Pallas kernels, local(): pl.pallas_call(pack_x_kernel, out_shape=(x_message, x_message), in_specs=...  1.06 us
  transfers between devices with their start and end apart: 4, of which 3 were waited for; matrix products, arithmetic and copies ran while one was open for 0% of the time, Pallas kernels for 19%

profile of v7, /device:TPU:0, one launch (start us, length us, event | category | flops | bytes accessed | tf_op | source)
XLA Modules:
  0.0 15.5 jit_solution(7472342557580337522)
XLA Ops:
  0.6 1.1 %pack_x.1 = (f32[80,128]{1,0:T(8,128)S(1)}, f32[80,128]{1,0:T(8,128)S(1)}) custom-call(f32[6,6,27,128]{3,2,1,0:T(8,128)} %bitcast.4, f32[3,3,27,64]{3,2,1,0:T(8,128)} %bitcast.7, s32[4,8]{1,0:T(4,128)} %level.3), custom_call_target="tpu_custom_call" | custom-call | tf_op jit(solution)/shard_map/pack_x/pallas_call | solution.py:685
  1.7 0.0 copy-start
  1.7 0.0 copy-start.1
  1.7 3.0 %collective-permute-start = (f32[80,128]{1,0:T(8,128)S(1)}, f32[80,128]{1,0:T(8,128)S(1)}, u32[]{:S(2)}, u32[]{:S(2)}) collective-permute-start(f32[80,128]{1,0:T(8,128)S(1)} %get-tuple-element.27), channel_id=1, source_target_pairs={{0,8},{8,16},{16,24},{24,0},{1,9},{9,17},{17,25},{25,1},{2,10},{10... | collective-permute-start | bytes 122888 | tf_op jit(solution)/shard_map/ppermute | solution.py:702
  4.7 1.0 %collective-permute-start.1 = (f32[80,128]{1,0:T(8,128)S(1)}, f32[80,128]{1,0:T(8,128)S(1)}, u32[]{:S(2)}, u32[]{:S(2)}) collective-permute-start(f32[80,128]{1,0:T(8,128)S(1)} %get-tuple-element.28), channel_id=1, source_target_pairs={{0,24},{8,0},{16,8},{24,16},{1,25},{9,1},{17,9},{25,17},{2,26},{10... | collective-permute-start | bytes 122888 | tf_op jit(solution)/shard_map/ppermute | solution.py:703
  5.8 0.0 copy-done
  5.8 0.0 copy-done.1
  5.8 1.8 %tables.1 = (s32[9,8,128]{2,1,0:T(8,128)S(1)}, f32[35,8,128]{2,1,0:T(8,128)S(1)}, s32[2,8,128]{2,1,0:T(8,128)S(1)}, s32[8,128]{1,0:T(8,128)S(1)}, f32[3,3,32,128...) custom-call(f32[6,6,27,128]{3,2,1,0:T(8,128)} %bitcast.5, ...), custom_call_target="tpu_custom_call" | custom-call | flops 10000000 | bytes 1000000 | tf_op jit(solution)/shard_map/tables/pallas_call | solution.py:706
  7.5 0.1 collective-permute-done.from_low
  7.7 1.1 %collective-permute-done.1.from_high = f32[80,128]{1,0:T(8,128)S(1)} collective-permute-done((f32[80,128]{1,0:T(8,128)S(1)}, f32[80,128]{1,0:T(8,128)S(1)}, u32[]{:S(2)}, u32[]{:S(2)}) %collective-permute-start.1) | collective-permute-done | bytes 40992 | tf_op jit(solution)/shard_map/ppermute | solution.py:703
  8.7 0.1 pack_y.1
  8.9 1.9 %collective-permute-start.2 = (f32[80,128]{1,0:T(8,128)S(1)}, f32[80,128]{1,0:T(8,128)S(1)}, u32[]{:S(2)}, u32[]{:S(2)}) collective-permute-start(f32[80,128]{1,0:T(8,128)S(1)} %get-tuple-element.30), channel_id=1, source_target_pairs={{0,7},{1,2},{2,1},{3,4},{4,3},{5,6},{6,5},{7,0},{8,15},{9,10},{10,... | collective-permute-start | bytes 122888 | tf_op jit(solution)/shard_map/ppermute | solution.py:738
  10.7 0.0 collective-permute-start.3
  10.7 1.2 %inner.1 = (f32[6,6,27,128]{3,2,1,0:T(8,128)}, f32[3,3,27,64]{3,2,1,0:T(8,128)}, f32[27,4,8,128]{3,2,1,0:T(8,128)S(1)}, f32[2,8,32,128]{3,2,1,0:T(8,128)S(1)}, f...) custom-call(f32[6,6,27,128]{3,2,1,0:T(8,128)S(1)} %get-tuple-element.25.fine, ...), custom_call_target="tpu_custom_call" | custom-call | flops 20000000 | bytes 1000000 | tf_op jit(solution)/shard_map/inner/pallas_call | solution.py:744
  11.9 2.3 %collective-permute-done.2.second = f32[80,128]{1,0:T(8,128)S(1)} collective-permute-done((f32[80,128]{1,0:T(8,128)S(1)}, f32[80,128]{1,0:T(8,128)S(1)}, u32[]{:S(2)}, u32[]{:S(2)}) %collective-permute-start.2) | collective-permute-done | bytes 40992 | tf_op jit(solution)/shard_map/ppermute | solution.py:738
  14.2 0.0 collective-permute-done.3.first
  14.2 1.3 %outer.1 = (f32[6,6,27,128]{3,2,1,0:T(8,128)}, f32[3,3,27,64]{3,2,1,0:T(8,128)}) custom-call(f32[80,128]{1,0:T(8,128)S(1)} %collective-permute-done.2.second, f32[80,128]{1,0:T(8,128)S(1)} %collective-permute-done.3.first, f32[27,2,8,128]{3,2,1,0:T(8,128)S(1)} %get-tuple-element.32.w_edge, ...), custom_call_target="tpu_custom_call", output_to_operand_aliasing={{0}: (13, {}), {1}: (14, {})} | custom-call | tf_op jit(solution)/shard_map/outer/pallas_call | solution.py:768
Async XLA Ops:
  1.7 4.1 %copy-start = (s32[4,8]{1,0:T(4,128)S(1)}, s32[4,8]{1,0:T(4,128)}, u32[]{:S(2)}) copy-start(s32[4,8]{1,0:T(4,128)} %level.3) | copy-start | bytes 388
  1.7 4.1 %copy-start.1 = (f32[27]{0:T(128)S(1)}, f32[27]{0:T(128)}, u32[]{:S(2)}) copy-start(f32[27]{0:T(128)} %rates.1) | copy-start | bytes 328
  1.7 6.0 %collective-permute-start = (f32[80,128]{1,0:T(8,128)S(1)}, f32[80,128]{1,0:T(8,128)S(1)}, u32[]{:S(2)}, u32[]{:S(2)}) collective-permute-start(f32[80,128]{1,0:T(8,128)S(1)} %get-tuple-element.27), channel_id=1, source_target_pairs={{0,8},{8,16},{16,24},{24,0},{1,9},{9,17},{17,25},{25,1},{2,10},{10... | collective-permute-start | bytes 122888 | tf_op jit(solution)/shard_map/ppermute | solution.py:702
  4.7 4.0 %collective-permute-start.1 = (f32[80,128]{1,0:T(8,128)S(1)}, f32[80,128]{1,0:T(8,128)S(1)}, u32[]{:S(2)}, u32[]{:S(2)}) collective-permute-start(f32[80,128]{1,0:T(8,128)S(1)} %get-tuple-element.28), channel_id=1, source_target_pairs={{0,24},{8,0},{16,8},{24,16},{1,25},{9,1},{17,9},{25,17},{2,26},{10... | collective-permute-start | bytes 122888 | tf_op jit(solution)/shard_map/ppermute | solution.py:703
  8.9 5.4 %collective-permute-start.2 = (f32[80,128]{1,0:T(8,128)S(1)}, f32[80,128]{1,0:T(8,128)S(1)}, u32[]{:S(2)}, u32[]{:S(2)}) collective-permute-start(f32[80,128]{1,0:T(8,128)S(1)} %get-tuple-element.30), channel_id=1, source_target_pairs={{0,7},{1,2},{2,1},{3,4},{4,3},{5,6},{6,5},{7,0},{8,15},{9,10},{10,... | collective-permute-start | bytes 122888 | tf_op jit(solution)/shard_map/ppermute | solution.py:738
  10.7 3.5 %collective-permute-start.3 = (f32[80,128]{1,0:T(8,128)S(1)}, f32[80,128]{1,0:T(8,128)S(1)}, u32[]{:S(2)}, u32[]{:S(2)}) collective-permute-start(f32[80,128]{1,0:T(8,128)S(1)} %get-tuple-element.31), channel_id=1, source_target_pairs={{0,1},{1,0},{2,3},{3,2},{4,5},{5,4},{6,7},{7,6},{8,9},{9,8},{10,11... | collective-permute-start | bytes 122888 | tf_op jit(solution)/shard_map/ppermute | solution.py:739
